TPU v7x, 32 devices: a whole 2x2x4 slice. The times are simulated.
32 devices in a mesh: dp: 4 (over x, core), center: 8 (over z, y).
Axes of the slice: x: 2, y: 2, z: 4, core: 2. Of those that a mesh axis runs over, the one named last changes fastest.
Arguments:
- features: bfloat16 [4096, 1024], P('dp'), may hold values from -6 to 6
- centers: bfloat16 [4096, 1024], P('center'), may hold values from -6 to 6
- targets: bfloat16 [4096, 256], P('dp'), may hold values from -6 to 6
Outputs:
- coef: float32 [4096, 256], P('center')
- residual: float32 [4096, 256], P('center')
All inputs are finite; a program needn't handle non-finite values.
Results may differ from a plain program's by a relative error of at most 0.024.
Values may be sent and summed in bfloat16 or wider, within the bound.
No kernel may reach another device: no remote copies, remote signals or barrier semaphores. Data moves between devices by JAX's collectives and lax.ppermute only.
A program may use at most 64 MiB of HBM per device.

v0:
```python
import functools
import math

import jax
import jax.numpy as jnp
from jax import lax
from jax.experimental import pallas as pl
from jax.experimental.pallas import tpu as pltpu
from jax.sharding import PartitionSpec as P


F32 = jnp.float32
BF16 = jnp.bfloat16
NT = (((1,), (1,)), ((), ()))
NN = (((1,), (0,)), ((), ()))
QUAD = 4
CORES = 2
TILE = 256


def vmem_call(body, outs, scratch=(), flops=0, nbytes=0, **kw):
    many = isinstance(outs, (list, tuple))
    return pl.pallas_call(
        body,
        out_shape=outs,
        scratch_shapes=list(scratch),
        out_specs=jax.tree.map(lambda _: pl.BlockSpec(memory_space=pltpu.VMEM), tuple(outs) if many else outs),
        compiler_params=pltpu.CompilerParams(vmem_limit_bytes=32 << 20),
        cost_estimate=pl.CostEstimate(flops=flops, bytes_accessed=nbytes, transcendentals=0),
        **kw,
    )


def kernel_block(rows, centers):
    scores = lax.dot_general(rows, centers, NT, preferred_element_type=F32)
    lifted = 1.0 + 0.5 / math.sqrt(rows.shape[1]) * scores
    return (lifted * lifted * lifted).astype(BF16)


def times_kernel(low, parts, emit):
    half = parts[0][0].shape[0]
    for part, refs in enumerate(parts):
        for at in range(0, half, TILE):
            total, first = None, 0
            for ref in refs:
                width = ref.shape[1]
                term = lax.dot_general(
                    ref[at : at + TILE, :], low[:, first : first + width], NT, preferred_element_type=F32
                )
                total = term if total is None else total + term
                first += width
            emit(slice(part * half + at, part * half + at + TILE), total.T)


def times_transposed(lows, parts, store):
    first = 0
    for one, two in zip(*parts):
        value = lax.dot_general(lows[0], one[...], NN, preferred_element_type=F32)
        value = value + lax.dot_general(lows[1], two[...], NN, preferred_element_type=F32)
        store(slice(first, first + one.shape[1]), value)
        first += one.shape[1]


def halves_of(refs):
    return refs[: len(refs) // 2], refs[len(refs) // 2 :]


def side_kernel(count, one, two, *refs):
    out = refs[count]

    def store(cols, value):
        out[:, cols] = value

    times_transposed((one[...], two[...]), halves_of(refs[:count]), store)


def early_kernel(scale, count, own, got, *refs):
    right_side, partial = refs[count:]
    value = (own[...] + got[...]) * scale
    right_side[...] = value

    def emit(cols, value):
        partial[:, cols] = value

    times_kernel(value.astype(BF16), halves_of(refs[:count]), emit)


def late_kernel(scale, count, own, got, early_side, early, *refs):
    right_side, partial, partial_low = refs[count:]
    value = (own[...] + got[...]) * scale
    before = early_side.shape[1]
    right_side[:, :before] = early_side[...]
    right_side[:, before:] = value

    def emit(cols, value):
        value = value + early[:, cols]
        partial[:, cols] = value
        partial_low[:, cols] = value.astype(BF16)

    times_kernel(value.astype(BF16), halves_of(refs[:count]), emit)


def back_kernel(last, count, partial, got, *refs):
    if last:
        image, image_low, squares = refs[count:]
    else:
        image, = refs[count:]
    total = partial[...] + got[...].astype(F32)
    low = total.astype(BF16)
    if last:
        sums = jnp.sum(total * low.astype(F32), axis=1, keepdims=True)
        squares[...] = jnp.broadcast_to(sums, squares.shape)

    def store(cols, value):
        image[:, cols] = value
        if last:
            image_low[:, cols] = value.astype(BF16)

    half = low.shape[1] // 2
    times_transposed((low[:, :half], low[:, half:]), halves_of(refs[:count]), store)


def sums_kernel(rows, own, got, right_side, image, sums):
    direction = right_side[...]
    value = (own[...] + got[...]) * (1.0 / rows) + 0.5 * direction
    image[...] = value
    for index, product in enumerate((direction * direction, direction * value, value * value)):
        sums[index] = jnp.broadcast_to(jnp.sum(product, axis=1, keepdims=True), sums.shape[1:])


def scalars(own_sums, got_sums):
    norm, curvature, image_sq = [own_sums[k][:, :1] + got_sums[k][:, :1] for k in range(3)]
    step = norm / (curvature + 1e-06)
    norm_next = norm - 2.0 * step * curvature + step * step * image_sq
    ratio = norm_next / (norm + 1e-06)
    direction_sq = norm_next + 2.0 * ratio * (norm - step * curvature) + ratio * ratio * norm
    return step, norm_next, ratio, direction_sq


def middle_kernel(count, own_sums, got_sums, right_side, image, *refs):
    residual, direction, partial, partial_low = refs[count:]
    step, _, ratio, _ = scalars(own_sums, got_sums)
    first = right_side[...]
    res = first - step * image[...]
    new = res + ratio * first
    residual[...] = res
    direction[...] = new

    def emit(cols, value):
        partial[:, cols] = value
        partial_low[:, cols] = value.astype(BF16)

    times_kernel(new.astype(BF16), halves_of(refs[:count]), emit)


def last_kernel(rows, own_sums, got_sums, own_sq, got_sq, own, got, right_side, residual, direction, *out):
    step, norm_next, _, direction_sq = scalars(own_sums, got_sums)
    curvature = (own_sq[:, :1] + got_sq[:, :1]) * (1.0 / rows) + 0.5 * direction_sq
    step_two = norm_next / (curvature + 1e-06)
    new = direction[...]
    image = (own[...] + got[...].astype(F32)) * (1.0 / rows) + 0.5 * new
    coef = (step * right_side[...] + step_two * new).astype(BF16)
    res = (residual[...] - step_two * image).astype(BF16)
    w = coef.shape[0]
    width = out[0].shape[1]
    for block in range(QUAD):
        out[block][0:w, :] = coef[:, block * width : (block + 1) * width]
        out[block][w : 2 * w, :] = res[:, block * width : (block + 1) * width]


def place_kernel(w, place, *refs):
    mine, other = refs[:QUAD], refs[QUAD : 2 * QUAD]
    coef, residual, coef_t, residual_t = refs[2 * QUAD :]
    core, quad = place[0], place[1]
    half = coef.shape[0] // CORES
    for hop in range(QUAD):
        group = jnp.bitwise_xor(quad, hop) * CORES
        for swapped, piece, at in ((0, mine[hop], group + core), (1, other[hop], group + 1 - core)):
            rows = pl.ds(pl.multiple_of(at * w, w), w)
            for index in range(CORES):
                to = index if hop == 0 else jnp.bitwise_xor(core, index ^ swapped)
                cols = pl.ds(pl.multiple_of(to * half, half), half)
                source = slice(index * half, (index + 1) * half)
                coef_t[rows, cols] = piece[0:w, source].astype(F32)
                residual_t[rows, cols] = piece[w : 2 * w, source].astype(F32)
    coef[...] = coef_t[...].T
    residual[...] = residual_t[...].T


def split_kernel(place, centers, mine, sem):
    half = mine.shape[0]
    at = pl.multiple_of(place[0] * half, half)
    copy = pltpu.make_async_copy(centers.at[pl.ds(at, half), :], mine, sem)
    copy.start()
    copy.wait()


def load_kernel(features, out, sem):
    copy = pltpu.make_async_copy(features, out, sem)
    copy.start()
    copy.wait()


def on_device(features, centers, targets):
    n_dp, n_center = lax.axis_size("dp"), lax.axis_size("center")
    chips, halves = n_dp // CORES, n_center // QUAD
    dp_at, center_at = lax.axis_index("dp"), lax.axis_index("center")
    core, quad = dp_at % CORES, center_at % QUAD
    examples, columns, block = features.shape[0], targets.shape[1], centers.shape[0]
    total_rows = examples * n_dp
    w = columns // (QUAD * CORES)
    half = block // CORES

    def swap(value):
        return lax.ppermute(value, "dp", [(i, i ^ 1) for i in range(n_dp)])

    def over_quad(value, hop):
        return lax.ppermute(value, "center", [(j, j ^ hop) for j in range(n_center)])

    def others(value, axis, size, inner):
        n = size * inner
        got = None
        for shift in range(1, size):
            pairs = [(i, (i // inner + shift) % size * inner + i % inner) for i in range(n)]
            piece = lax.ppermute(value, axis, pairs)
            got = piece if got is None else got + piece
        return got

    def over_x(value):
        return others(value, "dp", chips, CORES)

    def over_halves(value):
        return others(value, "center", halves, QUAD)

    sd = jax.ShapeDtypeStruct
    place = jnp.stack([core, quad]).astype(jnp.int32)
    depth = centers.shape[1]
    mine, = vmem_call(
        split_kernel,
        [sd((half, depth), BF16)],
        [pltpu.SemaphoreType.DMA(())],
        flops=1000000,
        in_specs=[pl.BlockSpec(memory_space=pltpu.SMEM), pl.BlockSpec(memory_space=pl.ANY)],
    )(place, centers)
    y_mine = over_quad(mine, 1)
    z_mine = over_quad(mine, 2)
    features_two = swap(features)
    features_two, = vmem_call(
        load_kernel,
        [sd(features.shape, BF16)],
        [pltpu.SemaphoreType.DMA(())],
        flops=1000000,
        in_specs=[pl.BlockSpec(memory_space=pl.ANY)],
    )(features_two)

    def pick(first):
        wanted = lax.broadcasted_iota(jnp.int32, (w, columns), 0) + first
        chosen = (wanted == lax.broadcasted_iota(jnp.int32, (w, columns), 1)).astype(BF16)
        return lax.dot_general(chosen, targets, NT, preferred_element_type=F32).astype(BF16)

    wanted_two = swap(pick((quad * CORES + 1 - core) * w))
    wanted = pick((quad * CORES + core) * w)

    def build(rows):
        return kernel_block(features, rows), kernel_block(features_two, rows)

    own = build(centers)
    pairs = []
    for i in range(n_dp):
        hop = 1 if i % CORES == 0 else 2
        pairs += [(i * n_center + j, i * n_center + (j ^ hop)) for j in range(n_center)]
    d_mine = lax.ppermute(jnp.where(core == 0, z_mine, y_mine), ("dp", "center"), pairs)
    y_other = swap(y_mine)
    z_other = swap(z_mine)
    y_0, z_0 = build(y_mine), build(z_mine)
    y_1, z_1 = build(y_other), build(z_other)
    early_pieces = [p[side] for side in range(2) for p in (own, y_0, y_1, z_0, z_1)]

    both, wide = CORES * examples, QUAD * block
    flops = 2 * 256 * both * wide
    side, = vmem_call(
        functools.partial(side_kernel, len(early_pieces)), [sd((w, wide - block), F32)], flops=flops * 3 // 4
    )(wanted, wanted_two, *early_pieces)
    got_side = over_x(side)
    d_other = swap(d_mine)
    d_0 = build(d_mine)
    d_1 = build(d_other)
    late_pieces = [p[side] for side in range(2) for p in (d_0, d_1)]
    late, = vmem_call(
        functools.partial(side_kernel, len(late_pieces)), [sd((w, block), F32)], flops=flops // 4
    )(wanted, wanted_two, *late_pieces)
    got_late = over_x(late)

    scale = 1.0 / math.sqrt(total_rows)
    early_side, early = vmem_call(
        functools.partial(early_kernel, scale, len(early_pieces)),
        [sd((w, wide - block), F32), sd((w, both), F32)],
        flops=flops * 3 // 4,
    )(side, got_side, *early_pieces)
    right_side, partial, partial_low = vmem_call(
        functools.partial(late_kernel, scale, len(late_pieces)),
        [sd((w, wide), F32), sd((w, both), F32), sd((w, both), BF16)],
        flops=flops // 4,
    )(late, got_late, early_side, early, *late_pieces)
    pieces = [
        piece for part in zip(halves_of(early_pieces), halves_of(late_pieces)) for group in part for piece in group
    ]
    count = len(pieces)
    got = over_halves(partial_low)
    image, = vmem_call(functools.partial(back_kernel, False, count), [sd((w, wide), F32)], flops=flops)(
        partial, got, *pieces
    )
    got = over_x(image)
    image, dots = vmem_call(
        functools.partial(sums_kernel, total_rows), [sd((w, wide), F32), sd((3, w, 128), F32)], flops=1000000
    )(image, got, right_side)
    got_dots = over_halves(dots)
    residual, direction, partial, partial_low = vmem_call(
        functools.partial(middle_kernel, count), [sd((w, wide), F32), sd((w, wide), F32), sd((w, both), F32), sd((w, both), BF16)], flops=flops
    )(dots, got_dots, right_side, image, *pieces)
    got = over_halves(partial_low)
    image, image_low, squares = vmem_call(
        functools.partial(back_kernel, True, count),
        [sd((w, wide), F32), sd((w, wide), BF16), sd((w, 128), F32)],
        flops=flops,
    )(partial, got, *pieces)
    got, got_squares = over_x(image_low), over_x(squares)
    finals = vmem_call(
        functools.partial(last_kernel, total_rows), [sd((2 * w, block), BF16)] * QUAD, flops=1000000
    )(dots, got_dots, squares, got_squares, image, got, right_side, residual, direction)
    landed = [finals[0]] + [over_quad(finals[hop], hop) for hop in range(1, QUAD)]
    landed_two = [swap(piece) for piece in landed]
    return tuple(
        vmem_call(
            functools.partial(place_kernel, w),
            [sd((block, columns), F32)] * 2,
            [pltpu.VMEM((columns, block), F32)] * 2,
            flops=1000000,
            in_specs=[pl.BlockSpec(memory_space=pltpu.SMEM)] + [pl.BlockSpec(memory_space=pltpu.VMEM)] * (2 * QUAD),
        )(place, *landed, *landed_two)
    )


def solution(mesh):
    placed = (P("dp", None), P("center", None), P("dp", None))
    return jax.shard_map(
        on_device,
        mesh=mesh,
        in_specs=placed,
        out_specs=(P("center", None), P("center", None)),
        check_vma=False,
    )
```

profile of v0, /device:TPU:0, one launch (start us, length us, event | category | flops | bytes accessed | tf_op | source)
XLA Modules:
  0.0 101.8 jit_solution(14186045936042322997)
XLA Ops:
  0.6 0.0 copy-start
  0.7 0.1 pad_add_fusion.place
  0.7 1.3 %copy-done.1 = bf16[512,1024]{1,0:T(8,128)(2,1)S(1)} copy-done((bf16[512,1024]{1,0:T(8,128)(2,1)S(1)}, bf16[512,1024]{1,0:T(8,128)(2,1)}, u32[]{:S(2)}) %copy-start.1) | copy-done | bytes 1048600
  2.0 0.6 shard_map.50
  2.6 3.1 %collective-permute-start.2 = (bf16[256,1024]{1,0:T(8,128)(2,1)S(1)}, bf16[256,1024]{1,0:T(8,128)(2,1)}, u32[]{:S(2)}, u32[]{:S(2)}) collective-permute-start(bf16[256,1024]{1,0:T(8,128)(2,1)S(1)} %shard_map.50), channel_id=1, source_target_pairs={{0,1},{1,0},{2,3},{3,2},{4,5},{5,4},{6,7},{7,6},{8,9},{9,8},{10,11... | collective-permute-start | bytes 1572872 | tf_op jit(solution)/shard_map/ppermute | solution.py:218
  5.7 1.6 %collective-permute-start.1 = (bf16[256,1024]{1,0:T(8,128)(2,1)S(1)}, bf16[256,1024]{1,0:T(8,128)(2,1)}, u32[]{:S(2)}, u32[]{:S(2)}) collective-permute-start(bf16[256,1024]{1,0:T(8,128)(2,1)S(1)} %shard_map.50), channel_id=1, source_target_pairs={{0,2},{1,3},{2,0},{3,1},{4,6},{5,7},{6,4},{7,5},{8,10},{9,11},{10,... | collective-permute-start | bytes 1572872 | tf_op jit(solution)/shard_map/ppermute | solution.py:218
  7.3 0.0 collective-permute-start.5
  7.3 0.2 convolution_convert_fusion
  7.5 0.5 collective-permute-start
  8.0 2.9 %fusion.refs_0_ = bf16[1024,512]{1,0:T(8,128)(2,1)S(1)} fusion(bf16[1024,1024]{1,0:T(8,128)(2,1)} %param.3, bf16[512,1024]{1,0:T(8,128)(2,1)S(1)} %copy-done.2), kind=kOutput, calls=%fused_computation.2 | convolution fusion | flops 1076363264 | bytes 4194304 | tf_op jit(solution)/shard_map/dot_general | solution.py:35
  11.0 0.2 convolution_convert_fusion.1.one
  11.2 6.5 %collective-permute-done.2 = bf16[256,1024]{1,0:T(8,128)(2,1)} collective-permute-done((bf16[256,1024]{1,0:T(8,128)(2,1)S(1)}, bf16[256,1024]{1,0:T(8,128)(2,1)}, u32[]{:S(2)}, u32[]{:S(2)}) %collective-permute-start.2) | collective-permute-done | bytes 524320 | tf_op jit(solution)/shard_map/ppermute | solution.py:218
  17.7 1.5 %collective-permute-done.1 = bf16[256,1024]{1,0:T(8,128)(2,1)} collective-permute-done((bf16[256,1024]{1,0:T(8,128)(2,1)S(1)}, bf16[256,1024]{1,0:T(8,128)(2,1)}, u32[]{:S(2)}, u32[]{:S(2)}) %collective-permute-start.1) | collective-permute-done | bytes 524320 | tf_op jit(solution)/shard_map/ppermute | solution.py:218
  19.2 1.1 %broadcast_select_fusion = bf16[256,1024]{1,0:T(8,128)(2,1)S(1)} fusion(bf16[256,1024]{1,0:T(8,128)(2,1)} %collective-permute-done.1, bf16[256,1024]{1,0:T(8,128)(2,1)} %collective-permute-done.2, pred[]{:T(512)S(6)} %eq.14), kind=kLoop, calls=%fused_computation.66 | loop fusion | flops 262144 | bytes 1572865 | tf_op jit(solution)/shard_map/jit(_where)/select_n | solution.py:272
  20.3 0.0 copy-start.3
  20.3 0.4 collective-permute-start.3
  20.7 0.5 collective-permute-start.8
  21.2 2.5 %fusion.30.refs_1_ = bf16[1024,256]{1,0:T(8,128)(2,1)S(1)} fusion(bf16[256,1024]{1,0:T(8,128)(2,1)} %collective-permute-done.2, bf16[1024,1024]{1,0:T(8,128)(2,1)} %param.3), kind=kOutput, calls=%fused_computation.56 | convolution fusion | flops 538181632 | bytes 3145728 | tf_op jit(solution)/shard_map/dot_general | solution.py:35
  23.8 1.8 %fusion.32.refs_3_ = bf16[1024,256]{1,0:T(8,128)(2,1)S(1)} fusion(bf16[256,1024]{1,0:T(8,128)(2,1)} %collective-permute-done.1, bf16[1024,1024]{1,0:T(8,128)(2,1)S(1)} %copy-done.3), kind=kOutput, calls=%fused_computation.58 | convolution fusion | flops 538181632 | bytes 3145728 | tf_op jit(solution)/shard_map/dot_general | solution.py:35
  25.6 4.0 %collective-permute-done.3 = bf16[256,1024]{1,0:T(8,128)(2,1)S(1)} collective-permute-done((bf16[256,1024]{1,0:T(8,128)(2,1)S(1)}, bf16[256,1024]{1,0:T(8,128)(2,1)S(1)}, u32[]{:S(2)}, u32[]{:S(2)}) %collective-permute-start.3) | collective-permute-done | bytes 524320 | tf_op jit(solution)/shard_map/ppermute | solution.py:272
  29.5 0.7 fusion.26.refs_0_.refs_5_
  30.3 0.7 fusion.31.refs_2_
  31.1 0.0 collective-permute-done.8
  31.1 0.7 fusion.33.refs_4_
  31.8 0.7 fusion.27.refs_1_.refs_6_
  32.6 1.6 %shard_map.51 = bf16[1024,1024]{1,0:T(8,128)(2,1)S(1)} custom-call(bf16[1024,1024]{1,0:T(8,128)(2,1)} %collective-permute-done.5.features), custom_call_target="tpu_custom_call" | custom-call | flops 1000000 | tf_op jit(solution)/shard_map/pallas_call | solution.py:248
  34.2 1.3 %fusion.1.refs_5_.refs_7_ = bf16[1024,512]{1,0:T(8,128)(2,1)S(1)} fusion(bf16[1024,1024]{1,0:T(8,128)(2,1)S(1)} %shard_map.51, bf16[512,1024]{1,0:T(8,128)(2,1)S(1)} %copy-done.2), kind=kOutput, calls=%fused_computation.3 | convolution fusion | flops 1076363264 | bytes 4194304 | tf_op jit(solution)/shard_map/dot_general | solution.py:35
  35.6 0.8 fusion.35.refs_7_.refs_9_
  36.3 0.8 fusion.37.refs_9_.refs_11_
  37.1 1.8 %fusion.34.refs_6_.refs_8_ = bf16[1024,256]{1,0:T(8,128)(2,1)S(1)} fusion(bf16[256,1024]{1,0:T(8,128)(2,1)} %collective-permute-done.2, bf16[1024,1024]{1,0:T(8,128)(2,1)S(1)} %shard_map.51), kind=kOutput, calls=%fused_computation.60 | convolution fusion | flops 538181632 | bytes 3145728 | tf_op jit(solution)/shard_map/dot_general | solution.py:35
  38.9 1.8 %fusion.36.refs_8_.refs_10_ = bf16[1024,256]{1,0:T(8,128)(2,1)S(1)} fusion(bf16[256,1024]{1,0:T(8,128)(2,1)} %collective-permute-done.1, bf16[1024,1024]{1,0:T(8,128)(2,1)S(1)} %shard_map.51), kind=kOutput, calls=%fused_computation.62 | convolution fusion | flops 538181632 | bytes 3145728 | tf_op jit(solution)/shard_map/dot_general | solution.py:35
  40.7 1.2 %shard_map.53.own = f32[32,1536]{1,0:T(8,128)S(1)} custom-call(bf16[32,1024]{1,0:T(8,128)(2,1)S(1)} %convolution_convert_fusion.1.one, bf16[32,1024]{1,0:T(8,128)(2,1)S(1)} %collective-permute-done.two, bf16[1024,512]{1,0:T(8,128)(2,1)S(1)} %fusion.refs_0_, bf16[1024,256]{1,0:T(8,128)(2,1)S(1)} %fusion.30.refs_1_, bf16[1024,256]{1,0:T(8,128)(2,1)S(1)} %fusion.31.refs_2_, ...), custom_call_target="tpu_custom_call" | custom-call | flops 1610612736 | tf_op jit(solution)/shard_map/pallas_call | solution.py:281
  41.8 1.5 %collective-permute-start.9 = (f32[32,1536]{1,0:T(8,128)S(1)}, f32[32,1536]{1,0:T(8,128)S(1)}, u32[]{:S(2)}, u32[]{:S(2)}) collective-permute-start(f32[32,1536]{1,0:T(8,128)S(1)} %shard_map.53.own), channel_id=1, source_target_pairs={{0,16},{8,24},{16,0},{24,8},{1,17},{9,25},{17,1},{25,9},{2,18},{10... | collective-permute-start | bytes 589832 | tf_op jit(solution)/shard_map/ppermute | solution.py:225
  43.4 0.7 fusion.29.refs_3_.refs_13_
  44.1 0.8 fusion.28.refs_2_.refs_12_
  44.9 0.6 shard_map.52.own
  45.5 0.5 collective-permute-start.6
  46.0 3.6 %collective-permute-done.9.got = f32[32,1536]{1,0:T(8,128)S(1)} collective-permute-done((f32[32,1536]{1,0:T(8,128)S(1)}, f32[32,1536]{1,0:T(8,128)S(1)}, u32[]{:S(2)}, u32[]{:S(2)}) %collective-permute-start.9) | collective-permute-done | bytes 196640 | tf_op jit(solution)/shard_map/ppermute | solution.py:225
  49.6 1.8 %shard_map.54 = (f32[32,1536]{1,0:T(8,128)S(1)}, f32[32,2048]{1,0:T(8,128)S(1)}) custom-call(f32[32,1536]{1,0:T(8,128)S(1)} %shard_map.53.own, f32[32,1536]{1,0:T(8,128)S(1)} %collective-permute-done.9.got, bf16[1024,512]{1,0:T(8,128)(2,1)S(1)} %fusion.refs_0_, bf16[1024,256]{1,0:T(8,128)(2,1)S(1)} %fusion.30.refs_1_, bf16[1024,256]{1,0:T(8,128)(2,1)S(1)} %fusion.31.refs_2_, ...), custom_call_target="tpu_custom_call" | custom-call | flops 1610612736 | tf_op jit(solution)/shard_map/pallas_call | solution.py:295
  51.5 0.8 shard_map.55
  52.3 2.6 %collective-permute-start.10 = (bf16[32,2048]{1,0:T(8,128)(2,1)S(1)}, bf16[32,2048]{1,0:T(8,128)(2,1)S(1)}, u32[]{:S(2)}, u32[]{:S(2)}) collective-permute-start(bf16[32,2048]{1,0:T(8,128)(2,1)S(1)} %get-tuple-element.23), channel_id=1, source_target_pairs={{0,4},{1,5},{2,6},{3,7},{4,0},{5,1},{6,2},{7,3},{8,12},{9,13},{10,... | collective-permute-start | bytes 393224 | tf_op jit(solution)/shard_map/ppermute | solution.py:225
  54.9 5.7 %collective-permute-done.10.got = bf16[32,2048]{1,0:T(8,128)(2,1)S(1)} collective-permute-done((bf16[32,2048]{1,0:T(8,128)(2,1)S(1)}, bf16[32,2048]{1,0:T(8,128)(2,1)S(1)}, u32[]{:S(2)}, u32[]{:S(2)}) %collective-permute-start.10) | collective-permute-done | bytes 131104 | tf_op jit(solution)/shard_map/ppermute | solution.py:225
  60.6 1.5 %shard_map.56.own = f32[32,2048]{1,0:T(8,128)S(1)} custom-call(f32[32,2048]{1,0:T(8,128)S(1)} %get-tuple-element.22.partial, bf16[32,2048]{1,0:T(8,128)(2,1)S(1)} %collective-permute-done.10.got, bf16[1024,512]{1,0:T(8,128)(2,1)S(1)} %fusion.refs_0_, bf16[1024,256]{1,0:T(8,128)(2,1)S(1)} %fusion.30.refs_1_, bf16[1024,256]{1,0:T(8,128)(2,1)S(1)} %fusion.31.refs_2_, ...), custom_call_target="tpu_custom_call" | custom-call | flops 2147483648 | tf_op jit(solution)/shard_map/pallas_call | solution.py:310
  62.1 1.5 %collective-permute-start.11 = (f32[32,2048]{1,0:T(8,128)S(1)}, f32[32,2048]{1,0:T(8,128)S(1)}, u32[]{:S(2)}, u32[]{:S(2)}) collective-permute-start(f32[32,2048]{1,0:T(8,128)S(1)} %shard_map.56.own), channel_id=1, source_target_pairs={{0,16},{8,24},{16,0},{24,8},{1,17},{9,25},{17,1},{25,9},{2,18},{10... | collective-permute-start | bytes 786440 | tf_op jit(solution)/shard_map/ppermute | solution.py:225
  63.6 5.7 %collective-permute-done.11.got = f32[32,2048]{1,0:T(8,128)S(1)} collective-permute-done((f32[32,2048]{1,0:T(8,128)S(1)}, f32[32,2048]{1,0:T(8,128)S(1)}, u32[]{:S(2)}, u32[]{:S(2)}) %collective-permute-start.11) | collective-permute-done | bytes 262176 | tf_op jit(solution)/shard_map/ppermute | solution.py:225
  69.4 0.2 shard_map.57
  69.5 0.0 collective-permute-start.12
  69.6 5.0 %collective-permute-done.12.got_sums = f32[3,32,128]{2,1,0:T(8,128)S(1)} collective-permute-done((f32[3,32,128]{2,1,0:T(8,128)S(1)}, f32[3,32,128]{2,1,0:T(8,128)S(1)}, u32[]{:S(2)}, u32[]{:S(2)}) %collective-permute-start.12) | collective-permute-done | bytes 49184 | tf_op jit(solution)/shard_map/ppermute | solution.py:225
  74.6 2.5 %shard_map.58 = (f32[32,2048]{1,0:T(8,128)S(1)}, f32[32,2048]{1,0:T(8,128)S(1)}, f32[32,2048]{1,0:T(8,128)S(1)}, bf16[32,2048]{1,0:T(8,128)(2,1)S(1)}) custom-call(f32[3,32,128]{2,1,0:T(8,128)S(1)} %get-tuple-element.25.own_sums, f32[3,32,128]{2,1,0:T(8,128)S(1)} %collective-permute-done.12.got_sums, f32[32,2048]{1,0:T(8,128)S(1)} %get-tuple-element.24.right_side, ...), custom_call_target="tpu_custom_call" | custom-call | flops 2147483648 | tf_op jit(solution)/shard_map/pallas_call | solution.py:318
  77.0 0.1 collective-permute-start.13
  77.1 7.3 %collective-permute-done.13.got = bf16[32,2048]{1,0:T(8,128)(2,1)S(1)} collective-permute-done((bf16[32,2048]{1,0:T(8,128)(2,1)S(1)}, bf16[32,2048]{1,0:T(8,128)(2,1)S(1)}, u32[]{:S(2)}, u32[]{:S(2)}) %collective-permute-start.13) | collective-permute-done | bytes 131104 | tf_op jit(solution)/shard_map/ppermute | solution.py:225
  84.4 1.5 %shard_map.59 = (f32[32,2048]{1,0:T(8,128)S(1)}, bf16[32,2048]{1,0:T(8,128)(2,1)S(1)}, f32[32,128]{1,0:T(8,128)S(1)}) custom-call(f32[32,2048]{1,0:T(8,128)S(1)} %get-tuple-element.27.partial, bf16[32,2048]{1,0:T(8,128)(2,1)S(1)} %collective-permute-done.13.got, bf16[1024,512]{1,0:T(8,128)(2,1)S(1)} %fusion.refs_0_, bf16[1024,256]{1,0:T(8,128)(2,1)S(1)} %fusion.30.refs_1_, ...), custom_call_target="tpu_custom_call" | custom-call | flops 2147483648 | tf_op jit(solution)/shard_map/pallas_call | solution.py:322
  85.9 1.5 %collective-permute-start.15 = (bf16[32,2048]{1,0:T(8,128)(2,1)S(1)}, bf16[32,2048]{1,0:T(8,128)(2,1)S(1)}, u32[]{:S(2)}, u32[]{:S(2)}) collective-permute-start(bf16[32,2048]{1,0:T(8,128)(2,1)S(1)} %get-tuple-element.31), channel_id=1, source_target_pairs={{0,16},{8,24},{16,0},{24,8},{1,17},{9,25},{17,1},{25,9},{2,18},{10... | collective-permute-start | bytes 393224 | tf_op jit(solution)/shard_map/ppermute | solution.py:225
  87.4 0.5 collective-permute-start.14
  87.9 3.2 %collective-permute-done.14.got_sq = f32[32,128]{1,0:T(8,128)S(1)} collective-permute-done((f32[32,128]{1,0:T(8,128)S(1)}, f32[32,128]{1,0:T(8,128)S(1)}, u32[]{:S(2)}, u32[]{:S(2)}) %collective-permute-start.14) | collective-permute-done | bytes 16416 | tf_op jit(solution)/shard_map/ppermute | solution.py:225
  91.1 0.2 shard_map.60
  91.4 0.6 collective-permute-start.16
  92.0 1.7 %collective-permute-start.17 = (bf16[64,512]{1,0:T(8,128)(2,1)S(1)}, bf16[64,512]{1,0:T(8,128)(2,1)S(1)}, u32[]{:S(2)}, u32[]{:S(2)}) collective-permute-start(bf16[64,512]{1,0:T(8,128)(2,1)S(1)} %get-tuple-element.36), channel_id=1, source_target_pairs={{0,2},{1,3},{2,0},{3,1},{4,6},{5,7},{6,4},{7,5},{8,10},{9,11},{10,... | collective-permute-start | bytes 196616 | tf_op jit(solution)/shard_map/ppermute | solution.py:218
  93.7 1.3 %collective-permute-start.18 = (bf16[64,512]{1,0:T(8,128)(2,1)S(1)}, bf16[64,512]{1,0:T(8,128)(2,1)S(1)}, u32[]{:S(2)}, u32[]{:S(2)}) collective-permute-start(bf16[64,512]{1,0:T(8,128)(2,1)S(1)} %get-tuple-element.37), channel_id=1, source_target_pairs={{0,3},{1,2},{2,1},{3,0},{4,7},{5,6},{6,5},{7,4},{8,11},{9,10},{10,... | collective-permute-start | bytes 196616 | tf_op jit(solution)/shard_map/ppermute | solution.py:218
  94.9 0.8 collective-permute-done.16.refs_1_
  95.7 0.6 collective-permute-done.17.refs_2_
  96.3 2.6 %collective-permute-done.18.refs_3_ = bf16[64,512]{1,0:T(8,128)(2,1)S(1)} collective-permute-done((bf16[64,512]{1,0:T(8,128)(2,1)S(1)}, bf16[64,512]{1,0:T(8,128)(2,1)S(1)}, u32[]{:S(2)}, u32[]{:S(2)}) %collective-permute-start.18) | collective-permute-done | bytes 65568 | tf_op jit(solution)/shard_map/ppermute | solution.py:218
  98.8 1.2 %collective-permute-done.22.refs_7_ = bf16[64,512]{1,0:T(8,128)(2,1)S(1)} collective-permute-done((bf16[64,512]{1,0:T(8,128)(2,1)S(1)}, bf16[64,512]{1,0:T(8,128)(2,1)S(1)}, u32[]{:S(2)}, u32[]{:S(2)}) %collective-permute-start.22) | collective-permute-done | bytes 65568 | tf_op jit(solution)/shard_map/ppermute | solution.py:215
  100.1 1.8 %shard_map.61 = (f32[512,256]{1,0:T(8,128)}, f32[512,256]{1,0:T(8,128)}) custom-call(s32[2]{0:T(128)S(1)} %pad_add_fusion.place, bf16[64,512]{1,0:T(8,128)(2,1)S(1)} %get-tuple-element.34.refs_0_, bf16[64,512]{1,0:T(8,128)(2,1)S(1)} %collective-permute-done.16.refs_1_, bf16[64,512]{1,0:T(8,128)(2,1)S(1)} %collective-permute-done.17.refs_2_, ...), custom_call_target="tpu_custom_call" | custom-call | flops 1000000 | tf_op jit(solution)/shard_map/pallas_call | solution.py:334
  (22 shorter events, 0.1 us)
Async XLA Ops:
  0.6 6.6 %copy-start = (bf16[1024,256]{1,0:T(8,128)(2,1)S(1)}, bf16[1024,256]{1,0:T(8,128)(2,1)}, u32[]{:S(2)}) copy-start(bf16[1024,256]{1,0:T(8,128)(2,1)} %param.5) | copy-start | bytes 1572868
  0.7 1.3 %copy-start.1 = (bf16[512,1024]{1,0:T(8,128)(2,1)S(1)}, bf16[512,1024]{1,0:T(8,128)(2,1)}, u32[]{:S(2)}) copy-start(bf16[512,1024]{1,0:T(8,128)(2,1)} %centers.1) | copy-start | bytes 3145732
  2.0 6.0 %copy-start.2 = (bf16[512,1024]{1,0:T(8,128)(2,1)S(1)}, bf16[512,1024]{1,0:T(8,128)(2,1)}, u32[]{:S(2)}) copy-start(bf16[512,1024]{1,0:T(8,128)(2,1)} %centers.1) | copy-start | bytes 3145732
  2.6 15.1 %collective-permute-start.2 = (bf16[256,1024]{1,0:T(8,128)(2,1)S(1)}, bf16[256,1024]{1,0:T(8,128)(2,1)}, u32[]{:S(2)}, u32[]{:S(2)}) collective-permute-start(bf16[256,1024]{1,0:T(8,128)(2,1)S(1)} %shard_map.50), channel_id=1, source_target_pairs={{0,1},{1,0},{2,3},{3,2},{4,5},{5,4},{6,7},{7,6},{8,9},{9,8},{10,11... | collective-permute-start | bytes 1572872 | tf_op jit(solution)/shard_map/ppermute | solution.py:218
  5.7 13.5 %collective-permute-start.1 = (bf16[256,1024]{1,0:T(8,128)(2,1)S(1)}, bf16[256,1024]{1,0:T(8,128)(2,1)}, u32[]{:S(2)}, u32[]{:S(2)}) collective-permute-start(bf16[256,1024]{1,0:T(8,128)(2,1)S(1)} %shard_map.50), channel_id=1, source_target_pairs={{0,2},{1,3},{2,0},{3,1},{4,6},{5,7},{6,4},{7,5},{8,10},{9,11},{10,... | collective-permute-start | bytes 1572872 | tf_op jit(solution)/shard_map/ppermute | solution.py:218
  7.3 25.3 %collective-permute-start.5 = (bf16[1024,1024]{1,0:T(8,128)(2,1)}, bf16[1024,1024]{1,0:T(8,128)(2,1)}, u32[]{:S(2)}, u32[]{:S(2)}) collective-permute-start(bf16[1024,1024]{1,0:T(8,128)(2,1)} %param.3), channel_id=1, source_target_pairs={{0,8},{8,0},{16,24},{24,16},{1,9},{9,1},{17,25},{25,17},{2,10},{10... | collective-permute-start | bytes 6291464 | tf_op jit(solution)/shard_map/ppermute | solution.py:215
  7.5 33.2 %collective-permute-start = (bf16[32,1024]{1,0:T(8,128)(2,1)S(1)}, bf16[32,1024]{1,0:T(8,128)(2,1)S(1)}, u32[]{:S(2)}, u32[]{:S(2)}) collective-permute-start(bf16[32,1024]{1,0:T(8,128)(2,1)S(1)} %convolution_convert_fusion), channel_id=1, source_target_pairs={{0,8},{8,0},{16,24},{24,16},{1,9},{9,1},{17,25},{25,17},{2,10},{10... | collective-permute-start | bytes 196616 | tf_op jit(solution)/shard_map/ppermute | solution.py:215
  20.3 3.5 %copy-start.3 = (bf16[1024,1024]{1,0:T(8,128)(2,1)S(1)}, bf16[1024,1024]{1,0:T(8,128)(2,1)}, u32[]{:S(2)}) copy-start(bf16[1024,1024]{1,0:T(8,128)(2,1)} %param.3) | copy-start | bytes 6291460
  20.3 9.2 %collective-permute-start.3 = (bf16[256,1024]{1,0:T(8,128)(2,1)S(1)}, bf16[256,1024]{1,0:T(8,128)(2,1)S(1)}, u32[]{:S(2)}, u32[]{:S(2)}) collective-permute-start(bf16[256,1024]{1,0:T(8,128)(2,1)S(1)} %broadcast_select_fusion), channel_id=1, source_target_pairs={{0,1},{1,0},{2,3},{3,2},{4,5},{5,4},{6,7},{7,6},{8,10},{9,11},{10,... | collective-permute-start | bytes 1572872 | tf_op jit(solution)/shard_map/ppermute | solution.py:272
  20.7 9.6 %collective-permute-start.7 = (bf16[256,1024]{1,0:T(8,128)(2,1)}, bf16[256,1024]{1,0:T(8,128)(2,1)S(1)}, u32[]{:S(2)}, u32[]{:S(2)}) collective-permute-start(bf16[256,1024]{1,0:T(8,128)(2,1)} %collective-permute-done.2), channel_id=1, source_target_pairs={{0,8},{8,0},{16,24},{24,16},{1,9},{9,1},{17,25},{25,17},{2,10},{10... | collective-permute-start | bytes 1572872 | tf_op jit(solution)/shard_map/ppermute | solution.py:215
  20.7 10.3 %collective-permute-start.8 = (bf16[256,1024]{1,0:T(8,128)(2,1)}, bf16[256,1024]{1,0:T(8,128)(2,1)S(1)}, u32[]{:S(2)}, u32[]{:S(2)}) collective-permute-start(bf16[256,1024]{1,0:T(8,128)(2,1)} %collective-permute-done.1), channel_id=1, source_target_pairs={{0,8},{8,0},{16,24},{24,16},{1,9},{9,1},{17,25},{25,17},{2,10},{10... | collective-permute-start | bytes 1572872 | tf_op jit(solution)/shard_map/ppermute | solution.py:215
  29.5 2.3 %collective-permute-start.4 = (bf16[256,1024]{1,0:T(8,128)(2,1)S(1)}, bf16[256,1024]{1,0:T(8,128)(2,1)S(1)}, u32[]{:S(2)}, u32[]{:S(2)}) collective-permute-start(bf16[256,1024]{1,0:T(8,128)(2,1)S(1)} %collective-permute-done.3), channel_id=1, source_target_pairs={{0,8},{8,0},{16,24},{24,16},{1,9},{9,1},{17,25},{25,17},{2,10},{10... | collective-permute-start | bytes 1572872 | tf_op jit(solution)/shard_map/ppermute | solution.py:215
  41.8 7.8 %collective-permute-start.9 = (f32[32,1536]{1,0:T(8,128)S(1)}, f32[32,1536]{1,0:T(8,128)S(1)}, u32[]{:S(2)}, u32[]{:S(2)}) collective-permute-start(f32[32,1536]{1,0:T(8,128)S(1)} %shard_map.53.own), channel_id=1, source_target_pairs={{0,16},{8,24},{16,0},{24,8},{1,17},{9,25},{17,1},{25,9},{2,18},{10... | collective-permute-start | bytes 589832 | tf_op jit(solution)/shard_map/ppermute | solution.py:225
  45.5 6.0 %collective-permute-start.6 = (f32[32,512]{1,0:T(8,128)S(1)}, f32[32,512]{1,0:T(8,128)S(1)}, u32[]{:S(2)}, u32[]{:S(2)}) collective-permute-start(f32[32,512]{1,0:T(8,128)S(1)} %shard_map.52.own), channel_id=1, source_target_pairs={{0,16},{8,24},{16,0},{24,8},{1,17},{9,25},{17,1},{25,9},{2,18},{10... | collective-permute-start | bytes 196616 | tf_op jit(solution)/shard_map/ppermute | solution.py:225
  52.3 8.4 %collective-permute-start.10 = (bf16[32,2048]{1,0:T(8,128)(2,1)S(1)}, bf16[32,2048]{1,0:T(8,128)(2,1)S(1)}, u32[]{:S(2)}, u32[]{:S(2)}) collective-permute-start(bf16[32,2048]{1,0:T(8,128)(2,1)S(1)} %get-tuple-element.23), channel_id=1, source_target_pairs={{0,4},{1,5},{2,6},{3,7},{4,0},{5,1},{6,2},{7,3},{8,12},{9,13},{10,... | collective-permute-start | bytes 393224 | tf_op jit(solution)/shard_map/ppermute | solution.py:225
  62.1 7.2 %collective-permute-start.11 = (f32[32,2048]{1,0:T(8,128)S(1)}, f32[32,2048]{1,0:T(8,128)S(1)}, u32[]{:S(2)}, u32[]{:S(2)}) collective-permute-start(f32[32,2048]{1,0:T(8,128)S(1)} %shard_map.56.own), channel_id=1, source_target_pairs={{0,16},{8,24},{16,0},{24,8},{1,17},{9,25},{17,1},{25,9},{2,18},{10... | collective-permute-start | bytes 786440 | tf_op jit(solution)/shard_map/ppermute | solution.py:225
  69.5 5.0 %collective-permute-start.12 = (f32[3,32,128]{2,1,0:T(8,128)S(1)}, f32[3,32,128]{2,1,0:T(8,128)S(1)}, u32[]{:S(2)}, u32[]{:S(2)}) collective-permute-start(f32[3,32,128]{2,1,0:T(8,128)S(1)} %get-tuple-element.25.own_sums), channel_id=1, source_target_pairs={{0,4},{1,5},{2,6},{3,7},{4,0},{5,1},{6,2},{7,3},{8,12},{9,13},{10,... | collective-permute-start | bytes 147464 | tf_op jit(solution)/shard_map/ppermute | solution.py:225
  77.0 7.3 %collective-permute-start.13 = (bf16[32,2048]{1,0:T(8,128)(2,1)S(1)}, bf16[32,2048]{1,0:T(8,128)(2,1)S(1)}, u32[]{:S(2)}, u32[]{:S(2)}) collective-permute-start(bf16[32,2048]{1,0:T(8,128)(2,1)S(1)} %get-tuple-element.28), channel_id=1, source_target_pairs={{0,4},{1,5},{2,6},{3,7},{4,0},{5,1},{6,2},{7,3},{8,12},{9,13},{10,... | collective-permute-start | bytes 393224 | tf_op jit(solution)/shard_map/ppermute | solution.py:225
  85.9 5.3 %collective-permute-start.15 = (bf16[32,2048]{1,0:T(8,128)(2,1)S(1)}, bf16[32,2048]{1,0:T(8,128)(2,1)S(1)}, u32[]{:S(2)}, u32[]{:S(2)}) collective-permute-start(bf16[32,2048]{1,0:T(8,128)(2,1)S(1)} %get-tuple-element.31), channel_id=1, source_target_pairs={{0,16},{8,24},{16,0},{24,8},{1,17},{9,25},{17,1},{25,9},{2,18},{10... | collective-permute-start | bytes 393224 | tf_op jit(solution)/shard_map/ppermute | solution.py:225
  87.4 3.7 %collective-permute-start.14 = (f32[32,128]{1,0:T(8,128)S(1)}, f32[32,128]{1,0:T(8,128)S(1)}, u32[]{:S(2)}, u32[]{:S(2)}) collective-permute-start(f32[32,128]{1,0:T(8,128)S(1)} %get-tuple-element.29.own_sq), channel_id=1, source_target_pairs={{0,16},{8,24},{16,0},{24,8},{1,17},{9,25},{17,1},{25,9},{2,18},{10... | collective-permute-start | bytes 49160 | tf_op jit(solution)/shard_map/ppermute | solution.py:225
  91.4 4.3 %collective-permute-start.16 = (bf16[64,512]{1,0:T(8,128)(2,1)S(1)}, bf16[64,512]{1,0:T(8,128)(2,1)S(1)}, u32[]{:S(2)}, u32[]{:S(2)}) collective-permute-start(bf16[64,512]{1,0:T(8,128)(2,1)S(1)} %get-tuple-element.35), channel_id=1, source_target_pairs={{0,1},{1,0},{2,3},{3,2},{4,5},{5,4},{6,7},{7,6},{8,9},{9,8},{10,11... | collective-permute-start | bytes 196616 | tf_op jit(solution)/shard_map/ppermute | solution.py:218
  92.0 4.3 %collective-permute-start.17 = (bf16[64,512]{1,0:T(8,128)(2,1)S(1)}, bf16[64,512]{1,0:T(8,128)(2,1)S(1)}, u32[]{:S(2)}, u32[]{:S(2)}) collective-permute-start(bf16[64,512]{1,0:T(8,128)(2,1)S(1)} %get-tuple-element.36), channel_id=1, source_target_pairs={{0,2},{1,3},{2,0},{3,1},{4,6},{5,7},{6,4},{7,5},{8,10},{9,11},{10,... | collective-permute-start | bytes 196616 | tf_op jit(solution)/shard_map/ppermute | solution.py:218
  93.7 5.2 %collective-permute-start.18 = (bf16[64,512]{1,0:T(8,128)(2,1)S(1)}, bf16[64,512]{1,0:T(8,128)(2,1)S(1)}, u32[]{:S(2)}, u32[]{:S(2)}) collective-permute-start(bf16[64,512]{1,0:T(8,128)(2,1)S(1)} %get-tuple-element.37), channel_id=1, source_target_pairs={{0,3},{1,2},{2,1},{3,0},{4,7},{5,6},{6,5},{7,4},{8,11},{9,10},{10,... | collective-permute-start | bytes 196616 | tf_op jit(solution)/shard_map/ppermute | solution.py:218
  94.9 3.9 %collective-permute-start.19 = (bf16[64,512]{1,0:T(8,128)(2,1)S(1)}, bf16[64,512]{1,0:T(8,128)(2,1)S(1)}, u32[]{:S(2)}, u32[]{:S(2)}) collective-permute-start(bf16[64,512]{1,0:T(8,128)(2,1)S(1)} %get-tuple-element.34.refs_0_), channel_id=1, source_target_pairs={{0,8},{8,0},{16,24},{24,16},{1,9},{9,1},{17,25},{25,17},{2,10},{10... | collective-permute-start | bytes 196616 | tf_op jit(solution)/shard_map/ppermute | solution.py:215
  95.7 3.1 %collective-permute-start.20 = (bf16[64,512]{1,0:T(8,128)(2,1)S(1)}, bf16[64,512]{1,0:T(8,128)(2,1)S(1)}, u32[]{:S(2)}, u32[]{:S(2)}) collective-permute-start(bf16[64,512]{1,0:T(8,128)(2,1)S(1)} %collective-permute-done.16.refs_1_), channel_id=1, source_target_pairs={{0,8},{8,0},{16,24},{24,16},{1,9},{9,1},{17,25},{25,17},{2,10},{10... | collective-permute-start | bytes 196616 | tf_op jit(solution)/shard_map/ppermute | solution.py:215
  96.3 2.6 %collective-permute-start.21 = (bf16[64,512]{1,0:T(8,128)(2,1)S(1)}, bf16[64,512]{1,0:T(8,128)(2,1)S(1)}, u32[]{:S(2)}, u32[]{:S(2)}) collective-permute-start(bf16[64,512]{1,0:T(8,128)(2,1)S(1)} %collective-permute-done.17.refs_2_), channel_id=1, source_target_pairs={{0,8},{8,0},{16,24},{24,16},{1,9},{9,1},{17,25},{25,17},{2,10},{10... | collective-permute-start | bytes 196616 | tf_op jit(solution)/shard_map/ppermute | solution.py:215
  98.8 1.3 %collective-permute-start.22 = (bf16[64,512]{1,0:T(8,128)(2,1)S(1)}, bf16[64,512]{1,0:T(8,128)(2,1)S(1)}, u32[]{:S(2)}, u32[]{:S(2)}) collective-permute-start(bf16[64,512]{1,0:T(8,128)(2,1)S(1)} %collective-permute-done.18.refs_3_), channel_id=1, source_target_pairs={{0,8},{8,0},{16,24},{24,16},{1,9},{9,1},{17,25},{25,17},{2,10},{10... | collective-permute-start | bytes 196616 | tf_op jit(solution)/shard_map/ppermute | solution.py:215
where the time goes:
time: 102 us
  waiting for transfers between devices  47.6 us (47%)
  matrix products  18.6 us (18%)
  starting transfers between devices  18 us (18%)
  Pallas kernels  14.3 us (14%)
  local copies, waits for them, and re-layouts  1.3 us (1%)
  other arithmetic  1.18 us (1%)
    ppermute x8, waiting for transfers between devices, others(): piece = lax.ppermute(value, axis, pairs)  30.5 us
    dot_general x14, matrix products, kernel_block(): scores = lax.dot_general(rows, centers, NT, preferred_element_type=F32)  18.2 us
    ppermute x5, waiting for transfers between devices, over_quad(): lax.ppermute(value, 'center', [(j, j ^ hop) for j in range(n_center)])  11.8 us
    ppermute x8, starting transfers between devices, others(): piece = lax.ppermute(value, axis, pairs)  8.32 us
    ppermute x5, starting transfers between devices, over_quad(): lax.ppermute(value, 'center', [(j, j ^ hop) for j in range(n_center)])  8.19 us
    ppermute x1, waiting for transfers between devices, on_device(): lax.ppermute(jnp.where(core == 0, z_mine, y_mine), ('dp', 'center'), pairs)  3.96 us
    pallas_call x1, Pallas kernels, on_device(): vmem_call(functools.partial(middle_kernel, count), [sd((w, wide), F32), s...  2.45 us
  transfers between devices with their start and end apart: 23, of which 13 were waited for; matrix products, arithmetic and copies ran while one was open for 19% of the time, Pallas kernels for 4%

commit v1 on v0

--- a/solution.py
+++ b/solution.py
@@ -16,16 +16,17 @@
 QUAD = 4
 CORES = 2
 TILE = 256
-
-
-def vmem_call(body, outs, scratch=(), flops=0, nbytes=0, **kw):
+CHUNKS = 2
+
+
+def vmem_call(body, outs, scratch=(), flops=0, nbytes=0, limit=32 << 20, **kw):
     many = isinstance(outs, (list, tuple))
     return pl.pallas_call(
         body,
         out_shape=outs,
         scratch_shapes=list(scratch),
         out_specs=jax.tree.map(lambda _: pl.BlockSpec(memory_space=pltpu.VMEM), tuple(outs) if many else outs),
-        compiler_params=pltpu.CompilerParams(vmem_limit_bytes=32 << 20),
+        compiler_params=pltpu.CompilerParams(vmem_limit_bytes=limit),
         cost_estimate=pl.CostEstimate(flops=flops, bytes_accessed=nbytes, transcendentals=0),
         **kw,
     )
@@ -74,30 +75,52 @@
     times_transposed((one[...], two[...]), halves_of(refs[:count]), store)
 
 
-def early_kernel(scale, count, own, got, *refs):
-    right_side, partial = refs[count:]
-    value = (own[...] + got[...]) * scale
-    right_side[...] = value
+def right_kernel(scale, own, got, *out):
+    w = out[0].shape[0]
+    for hop in range(QUAD):
+        rows = slice(hop * w, (hop + 1) * w)
+        out[hop][...] = (own[rows, :] + got[rows, :]) * scale
+
+
+def segments():
+    found = []
+    for chunk in range(CHUNKS):
+        for far in range(CORES):
+            found += [(1, far, chunk), (2, far, chunk)]
+    for far in range(CORES):
+        found += [(3, far, chunk) for chunk in range(CHUNKS)]
+    return found
+
+
+def early_kernel(count, n_early, *refs):
+    sides, k_refs = refs[:QUAD], refs[QUAD : QUAD + count]
+    right_side, low_last, partial = refs[QUAD + count :]
+    core = lax.axis_index("dp") % CORES
+    width = sides[0].shape[1]
+    half = width // CORES
+    cut = half // CHUNKS
+    right_side[:, :width] = sides[0][...]
+    for index, (hop, far, chunk) in enumerate(segments()):
+        at = pl.multiple_of(jnp.bitwise_xor(core, far) * half + chunk * cut, cut)
+        to = width + index * cut
+        right_side[:, to : to + cut] = sides[hop][:, pl.ds(at, cut)]
+    low_last[...] = right_side[:, n_early:].astype(BF16)
 
     def emit(cols, value):
         partial[:, cols] = value
 
-    times_kernel(value.astype(BF16), halves_of(refs[:count]), emit)
-
-
-def late_kernel(scale, count, own, got, early_side, early, *refs):
-    right_side, partial, partial_low = refs[count:]
-    value = (own[...] + got[...]) * scale
-    before = early_side.shape[1]
-    right_side[:, :before] = early_side[...]
-    right_side[:, before:] = value
+    times_kernel(right_side[:, :n_early].astype(BF16), halves_of(k_refs), emit)
+
+
+def late_kernel(count, low, early, *refs):
+    partial, partial_low = refs[count:]
 
     def emit(cols, value):
         value = value + early[:, cols]
         partial[:, cols] = value
         partial_low[:, cols] = value.astype(BF16)
 
-    times_kernel(value.astype(BF16), halves_of(refs[:count]), emit)
+    times_kernel(low, halves_of(refs[:count]), emit)
 
 
 def back_kernel(last, count, partial, got, *refs):
@@ -163,9 +186,14 @@
     res = (residual[...] - step_two * image).astype(BF16)
     w = coef.shape[0]
     width = out[0].shape[1]
-    for block in range(QUAD):
-        out[block][0:w, :] = coef[:, block * width : (block + 1) * width]
-        out[block][w : 2 * w, :] = res[:, block * width : (block + 1) * width]
+    half = width // CORES
+    cut = half // CHUNKS
+    for first, value in ((0, coef), (w, res)):
+        rows = slice(first, first + w)
+        out[0][rows, :] = value[:, :width]
+        for index, (hop, far, chunk) in enumerate(segments()):
+            at, to = width + index * cut, far * half + chunk * cut
+            out[hop][rows, to : to + cut] = value[:, at : at + cut]
 
 
 def place_kernel(w, place, *refs):
@@ -187,18 +215,59 @@
     residual[...] = residual_t[...].T
 
 
-def split_kernel(place, centers, mine, sem):
-    half = mine.shape[0]
-    at = pl.multiple_of(place[0] * half, half)
-    copy = pltpu.make_async_copy(centers.at[pl.ds(at, half), :], mine, sem)
-    copy.start()
-    copy.wait()
-
-
-def load_kernel(features, out, sem):
-    copy = pltpu.make_async_copy(features, out, sem)
-    copy.start()
-    copy.wait()
+def run(copies):
+    for copy in copies:
+        copy.start()
+    for copy in copies:
+        copy.wait()
+
+
+def split_kernel(centers, *refs):
+    chunks, sems = refs[:-1], refs[-1]
+    cut = chunks[0].shape[0]
+    at = (lax.axis_index("dp") % CORES) * (cut * CHUNKS)
+    run(
+        [
+            pltpu.make_async_copy(centers.at[pl.ds(pl.multiple_of(at + k * cut, cut), cut), :], chunk, sems.at[k])
+            for k, chunk in enumerate(chunks)
+        ]
+    )
+
+
+def keep_kernel(value, out, sem):
+    run([pltpu.make_async_copy(value, out, sem)])
+
+
+def fork_kernel(y, z, both, send, sems):
+    cut = y.shape[0]
+    copies = [
+        pltpu.make_async_copy(y, both.at[pl.ds(0, cut), :], sems.at[0]),
+        pltpu.make_async_copy(z, both.at[pl.ds(cut, cut), :], sems.at[1]),
+    ]
+    for copy in copies:
+        copy.start()
+    core = lax.axis_index("dp") % CORES
+
+    @pl.when(core == 0)
+    def _():
+        run([pltpu.make_async_copy(z, send, sems.at[2])])
+
+    @pl.when(core != 0)
+    def _():
+        run([pltpu.make_async_copy(y, send, sems.at[2])])
+
+    for copy in copies:
+        copy.wait()
+
+
+def join_kernel(a, b, both, sems):
+    cut = a.shape[0]
+    run(
+        [
+            pltpu.make_async_copy(a, both.at[pl.ds(0, cut), :], sems.at[0]),
+            pltpu.make_async_copy(b, both.at[pl.ds(cut, cut), :], sems.at[1]),
+        ]
+    )
 
 
 def on_device(features, centers, targets):
@@ -235,73 +304,93 @@
     sd = jax.ShapeDtypeStruct
     place = jnp.stack([core, quad]).astype(jnp.int32)
     depth = centers.shape[1]
-    mine, = vmem_call(
+    mine_size = half * depth
+    any_space = pl.BlockSpec(memory_space=pl.ANY)
+    cut = half // CHUNKS
+    chunks = vmem_call(
         split_kernel,
-        [sd((half, depth), BF16)],
+        [sd((cut, depth), BF16)] * CHUNKS,
+        [pltpu.SemaphoreType.DMA((CHUNKS,))],
+        flops=1000000,
+        limit=(64 << 20) - 2 * (mine_size + targets.size) - (1 << 19),
+        in_specs=[any_space],
+    )(centers)
+    y_in, z_in = [], []
+    for k in range(CHUNKS):
+        y_in.append(over_quad(chunks[k], 1))
+        z_in.append(over_quad(chunks[k], 2))
+    features_two = swap(features)
+    features_two, = vmem_call(
+        keep_kernel,
+        [pltpu.VMEM(features.shape, BF16)],
         [pltpu.SemaphoreType.DMA(())],
         flops=1000000,
-        in_specs=[pl.BlockSpec(memory_space=pltpu.SMEM), pl.BlockSpec(memory_space=pl.ANY)],
-    )(place, centers)
-    y_mine = over_quad(mine, 1)
-    z_mine = over_quad(mine, 2)
-    features_two = swap(features)
-    features_two, = vmem_call(
-        load_kernel,
-        [sd(features.shape, BF16)],
-        [pltpu.SemaphoreType.DMA(())],
-        flops=1000000,
-        in_specs=[pl.BlockSpec(memory_space=pl.ANY)],
+        in_specs=[any_space],
     )(features_two)
 
-    def pick(first):
-        wanted = lax.broadcasted_iota(jnp.int32, (w, columns), 0) + first
-        chosen = (wanted == lax.broadcasted_iota(jnp.int32, (w, columns), 1)).astype(BF16)
+    def pick(of_core):
+        row = lax.broadcasted_iota(jnp.int32, (QUAD * w, columns), 0)
+        wanted = ((quad ^ (row // w)) * CORES + of_core) * w + row % w
+        chosen = (wanted == lax.broadcasted_iota(jnp.int32, (QUAD * w, columns), 1)).astype(BF16)
         return lax.dot_general(chosen, targets, NT, preferred_element_type=F32).astype(BF16)
 
-    wanted_two = swap(pick((quad * CORES + 1 - core) * w))
-    wanted = pick((quad * CORES + core) * w)
+    wanted_two = swap(pick(1 - core))
+    wanted = pick(core)
 
     def build(rows):
         return kernel_block(features, rows), kernel_block(features_two, rows)
 
     own = build(centers)
+    both, wide = CORES * examples, QUAD * block
+    flops = 2 * 256 * both * wide
+    side, = vmem_call(functools.partial(side_kernel, 2), [sd((QUAD * w, block), F32)], flops=flops // 4)(
+        wanted, wanted_two, *own
+    )
+    got_side = over_x(side)
     pairs = []
     for i in range(n_dp):
         hop = 1 if i % CORES == 0 else 2
         pairs += [(i * n_center + j, i * n_center + (j ^ hop)) for j in range(n_center)]
-    d_mine = lax.ppermute(jnp.where(core == 0, z_mine, y_mine), ("dp", "center"), pairs)
-    y_other = swap(y_mine)
-    z_other = swap(z_mine)
-    y_0, z_0 = build(y_mine), build(z_mine)
-    y_1, z_1 = build(y_other), build(z_other)
-    early_pieces = [p[side] for side in range(2) for p in (own, y_0, y_1, z_0, z_1)]
-
-    both, wide = CORES * examples, QUAD * block
-    flops = 2 * 256 * both * wide
-    side, = vmem_call(
-        functools.partial(side_kernel, len(early_pieces)), [sd((w, wide - block), F32)], flops=flops * 3 // 4
-    )(wanted, wanted_two, *early_pieces)
-    got_side = over_x(side)
-    d_other = swap(d_mine)
-    d_0 = build(d_mine)
-    d_1 = build(d_other)
+    early_groups, d_in = [own], []
+    for k in range(CHUNKS):
+        near, d_send = vmem_call(
+            fork_kernel,
+            [pltpu.VMEM((2 * cut, depth), BF16), pltpu.VMEM((cut, depth), BF16)],
+            [pltpu.SemaphoreType.DMA((3,))],
+            flops=1000000,
+            in_specs=[any_space] * 2,
+        )(y_in[k], z_in[k])
+        d_in.append(lax.ppermute(d_send, ("dp", "center"), pairs))
+        far = swap(near)
+        early_groups.append(build(near))
+        early_groups.append(build(far))
+    sides = vmem_call(
+        functools.partial(right_kernel, 1.0 / math.sqrt(total_rows)), [sd((w, block), F32)] * QUAD, flops=1000000
+    )(side, got_side)
+    sides = [sides[0]] + [over_quad(sides[hop], hop) for hop in range(1, QUAD)]
+    early_pieces = [p[side] for side in range(2) for p in early_groups]
+    d_near, = vmem_call(
+        join_kernel,
+        [pltpu.VMEM((half, depth), BF16)],
+        [pltpu.SemaphoreType.DMA((2,))],
+        flops=1000000,
+        in_specs=[any_space] * 2,
+    )(*d_in)
+    d_far = swap(d_near)
+    d_0 = build(d_near)
+    d_1 = build(d_far)
     late_pieces = [p[side] for side in range(2) for p in (d_0, d_1)]
-    late, = vmem_call(
-        functools.partial(side_kernel, len(late_pieces)), [sd((w, block), F32)], flops=flops // 4
-    )(wanted, wanted_two, *late_pieces)
-    got_late = over_x(late)
-
-    scale = 1.0 / math.sqrt(total_rows)
-    early_side, early = vmem_call(
-        functools.partial(early_kernel, scale, len(early_pieces)),
-        [sd((w, wide - block), F32), sd((w, both), F32)],
+    count = len(early_pieces)
+    right_side, low_last, early = vmem_call(
+        functools.partial(early_kernel, count, wide - block),
+        [sd((w, wide), F32), sd((w, block), BF16), sd((w, both), F32)],
         flops=flops * 3 // 4,
-    )(side, got_side, *early_pieces)
-    right_side, partial, partial_low = vmem_call(
-        functools.partial(late_kernel, scale, len(late_pieces)),
-        [sd((w, wide), F32), sd((w, both), F32), sd((w, both), BF16)],
+    )(*sides, *early_pieces)
+    partial, partial_low = vmem_call(
+        functools.partial(late_kernel, len(late_pieces)),
+        [sd((w, both), F32), sd((w, both), BF16)],
         flops=flops // 4,
-    )(late, got_late, early_side, early, *late_pieces)
+    )(low_last, early, *late_pieces)
     pieces = [
         piece for part in zip(halves_of(early_pieces), halves_of(late_pieces)) for group in part for piece in group
     ]

time: 102 us -> 104 us (1.020)
  starting transfers between devices: 18 us -> 24.1 us
  matrix products: 18.6 us -> 15.8 us
  local copies, waits for them, and re-layouts: 1.3 us -> 0.16 us
  other arithmetic: 1.18 us -> 0.09 us
    ppermute x5 -> x10, starting transfers between devices: 8.19 us -> 12.3 us  [over_quad(): lax.ppermute(value, 'center', [(j, j ^ hop) for j in range(n_center)])]
    dot_general x14, matrix products: 18.2 us -> 15.1 us  [kernel_block(): scores = lax.dot_general(rows, centers, NT, preferred_element_type=F32)]
    ppermute x1 -> x2, starting transfers between devices: 0.42 us -> 2.09 us  [on_device(): d_in.append(lax.ppermute(d_send, ('dp', 'center'), pairs))]
    ppermute x8 -> x7, waiting for transfers between devices: 30.5 us -> 29 us  [others(): piece = lax.ppermute(value, axis, pairs)]
    ppermute x5 -> x10, waiting for transfers between devices: 11.8 us -> 13.3 us  [over_quad(): lax.ppermute(value, 'center', [(j, j ^ hop) for j in range(n_center)])]
    ppermute x8 -> x7, starting transfers between devices: 8.32 us -> 9.58 us  [others(): piece = lax.ppermute(value, axis, pairs)]
    unnamed x8 -> x6, local copies, waits for them, and re-layouts: 1.3 us -> 0.16 us
    select_n x1 -> x0, other arithmetic: 1.1 us -> none  [on_device(): jnp.where(core == 0, z_mine, y_mine)]
  transfers between devices with their start and end apart: 23 -> 28, of which waited for: 13 -> 18; matrix products, arithmetic and copies ran while one was open for 19% -> 15% of each run, Pallas kernels for 4% -> 2%
where the time goes in v1:
time: 104 us; the launch traced here: 103 us
  waiting for transfers between devices  47.3 us (45%)
  starting transfers between devices  24.1 us (23%)
  matrix products  15.8 us (15%)
  Pallas kernels  15 us (14%)
    ppermute x7, waiting for transfers between devices, others(): piece = lax.ppermute(value, axis, pairs)  29 us
    dot_general x14, matrix products, kernel_block(): scores = lax.dot_general(rows, centers, NT, preferred_element_type=F32)  15.1 us
    ppermute x10, waiting for transfers between devices, over_quad(): lax.ppermute(value, 'center', [(j, j ^ hop) for j in range(n_center)])  13.3 us
    ppermute x10, starting transfers between devices, over_quad(): lax.ppermute(value, 'center', [(j, j ^ hop) for j in range(n_center)])  12.3 us
    ppermute x7, starting transfers between devices, others(): piece = lax.ppermute(value, axis, pairs)  9.58 us
    ppermute x2, waiting for transfers between devices, on_device(): d_in.append(lax.ppermute(d_send, ('dp', 'center'), pairs))  3.85 us
    pallas_call x1, Pallas kernels, on_device(): vmem_call(functools.partial(middle_kernel, count), [sd((w, wide), F32), s...  2.68 us
    ppermute x2, starting transfers between devices, on_device(): d_in.append(lax.ppermute(d_send, ('dp', 'center'), pairs))  2.09 us
  transfers between devices with their start and end apart: 28, of which 18 were waited for; matrix products, arithmetic and copies ran while one was open for 15% of the time, Pallas kernels for 2%

profile of v1, /device:TPU:0, one launch (start us, length us, event | category | flops | bytes accessed | tf_op | source)
XLA Modules:
  0.0 103.4 jit_solution(17966065705722758868)
XLA Ops:
  0.6 1.9 %shard_map.53 = (bf16[128,1024]{1,0:T(8,128)(2,1)}, bf16[128,1024]{1,0:T(8,128)(2,1)}) custom-call(bf16[512,1024]{1,0:T(8,128)(2,1)} %centers.1), custom_call_target="tpu_custom_call" | custom-call | flops 1000000 | tf_op jit(solution)/shard_map/pallas_call | solution.py:310
  2.6 3.1 %collective-permute-start.6 = (bf16[128,1024]{1,0:T(8,128)(2,1)}, bf16[128,1024]{1,0:T(8,128)(2,1)S(1)}, u32[]{:S(2)}, u32[]{:S(2)}) collective-permute-start(bf16[128,1024]{1,0:T(8,128)(2,1)} %get-tuple-element.34), channel_id=1, source_target_pairs={{0,1},{1,0},{2,3},{3,2},{4,5},{5,4},{6,7},{7,6},{8,9},{9,8},{10,11... | collective-permute-start | bytes 786440 | tf_op jit(solution)/shard_map/ppermute | solution.py:287
  5.6 1.6 %collective-permute-start.7 = (bf16[128,1024]{1,0:T(8,128)(2,1)}, bf16[128,1024]{1,0:T(8,128)(2,1)S(1)}, u32[]{:S(2)}, u32[]{:S(2)}) collective-permute-start(bf16[128,1024]{1,0:T(8,128)(2,1)} %get-tuple-element.34), channel_id=1, source_target_pairs={{0,2},{1,3},{2,0},{3,1},{4,6},{5,7},{6,4},{7,5},{8,10},{9,11},{10,... | collective-permute-start | bytes 786440 | tf_op jit(solution)/shard_map/ppermute | solution.py:287
  7.2 0.4 collective-permute-start.10
  7.8 3.2 %fusion.refs_0_.refs_4_ = bf16[1024,512]{1,0:T(8,128)(2,1)S(1)} fusion(bf16[1024,1024]{1,0:T(8,128)(2,1)} %param.3, bf16[512,1024]{1,0:T(8,128)(2,1)} %centers.1), kind=kOutput, calls=%fused_computation.2 | convolution fusion | flops 1076363264 | bytes 4194304 | tf_op jit(solution)/shard_map/dot_general | solution.py:36
  11.0 0.3 convolution_convert_fusion.1.one
  11.3 0.3 convolution_convert_fusion
  11.7 1.3 %collective-permute-done.6.y = bf16[128,1024]{1,0:T(8,128)(2,1)S(1)} collective-permute-done((bf16[128,1024]{1,0:T(8,128)(2,1)}, bf16[128,1024]{1,0:T(8,128)(2,1)S(1)}, u32[]{:S(2)}, u32[]{:S(2)}) %collective-permute-start.6) | collective-permute-done | bytes 262176 | tf_op jit(solution)/shard_map/ppermute | solution.py:287
  13.0 2.0 %collective-permute-done.7.z = bf16[128,1024]{1,0:T(8,128)(2,1)S(1)} collective-permute-done((bf16[128,1024]{1,0:T(8,128)(2,1)}, bf16[128,1024]{1,0:T(8,128)(2,1)S(1)}, u32[]{:S(2)}, u32[]{:S(2)}) %collective-permute-start.7) | collective-permute-done | bytes 262176 | tf_op jit(solution)/shard_map/ppermute | solution.py:287
  15.2 4.0 %collective-permute-done.10.z = bf16[128,1024]{1,0:T(8,128)(2,1)S(1)} collective-permute-done((bf16[128,1024]{1,0:T(8,128)(2,1)}, bf16[128,1024]{1,0:T(8,128)(2,1)S(1)}, u32[]{:S(2)}, u32[]{:S(2)}) %collective-permute-start.10) | collective-permute-done | bytes 262176 | tf_op jit(solution)/shard_map/ppermute | solution.py:287
  19.2 0.4 collective-permute-start.12
  19.7 1.7 %collective-permute-start.13 = (bf16[128,1024]{1,0:T(8,128)(2,1)S(1)}, bf16[128,1024]{1,0:T(8,128)(2,1)S(1)}, u32[]{:S(2)}, u32[]{:S(2)}) collective-permute-start(bf16[128,1024]{1,0:T(8,128)(2,1)S(1)} %get-tuple-element.41), channel_id=1, source_target_pairs={{0,1},{1,0},{2,3},{3,2},{4,5},{5,4},{6,7},{7,6},{8,10},{9,11},{10,... | collective-permute-start | bytes 786440 | tf_op jit(solution)/shard_map/ppermute | solution.py:363
  21.4 2.3 %fusion.26.refs_5_.refs_1_ = bf16[1024,256]{1,0:T(8,128)(2,1)S(1)} fusion(bf16[256,1024]{1,0:T(8,128)(2,1)S(1)} %get-tuple-element.35, bf16[1024,1024]{1,0:T(8,128)(2,1)} %param.3), kind=kOutput, calls=%fused_computation.52 | convolution fusion | flops 538181632 | bytes 3145728 | tf_op jit(solution)/shard_map/dot_general | solution.py:36
  23.8 0.7 fusion.28.refs_7_.refs_3_
  24.5 1.0 %collective-permute-done.12.a = bf16[128,1024]{1,0:T(8,128)(2,1)S(1)} collective-permute-done((bf16[128,1024]{1,0:T(8,128)(2,1)S(1)}, bf16[128,1024]{1,0:T(8,128)(2,1)S(1)}, u32[]{:S(2)}, u32[]{:S(2)}) %collective-permute-start.12) | collective-permute-done | bytes 262176 | tf_op jit(solution)/shard_map/ppermute | solution.py:363
  25.6 2.8 %collective-permute-done.13.b = bf16[128,1024]{1,0:T(8,128)(2,1)S(1)} collective-permute-done((bf16[128,1024]{1,0:T(8,128)(2,1)S(1)}, bf16[128,1024]{1,0:T(8,128)(2,1)S(1)}, u32[]{:S(2)}, u32[]{:S(2)}) %collective-permute-start.13) | collective-permute-done | bytes 262176 | tf_op jit(solution)/shard_map/ppermute | solution.py:363
  28.4 0.2 shard_map.57
  28.7 0.8 fusion.34.refs_0_.refs_5_
  29.5 0.7 fusion.27.refs_6_.refs_2_
  30.2 0.7 fusion.29.refs_8_.refs_4_
  31.0 0.7 fusion.35.refs_1_.refs_6_
  31.8 1.7 %shard_map.50 = bf16[1024,1024]{1,0:T(8,128)(2,1)S(1)} custom-call(bf16[1024,1024]{1,0:T(8,128)(2,1)} %collective-permute-done.1.value), custom_call_target="tpu_custom_call" | custom-call | flops 1000000 | tf_op jit(solution)/shard_map/pallas_call | solution.py:323
  33.5 0.1 copy-done.1
  33.6 1.3 %fusion.1.refs_1_.refs_9_.refs_7_ = bf16[1024,512]{1,0:T(8,128)(2,1)S(1)} fusion(bf16[1024,1024]{1,0:T(8,128)(2,1)S(1)} %shard_map.50, bf16[512,1024]{1,0:T(8,128)(2,1)S(1)} %copy-done.1), kind=kOutput, calls=%fused_computation.3 | convolution fusion | flops 1076363264 | bytes 4194304 | tf_op jit(solution)/shard_map/dot_general | solution.py:36
  35.0 0.7 fusion.30.refs_10_.refs_8_
  35.7 0.8 fusion.32.refs_12_.refs_10_
  36.5 0.8 fusion.36.refs_2_.refs_12_
  37.3 0.4 shard_map.51.own
  37.7 1.6 %collective-permute-start.2 = (f32[128,512]{1,0:T(8,128)S(1)}, f32[128,512]{1,0:T(8,128)S(1)}, u32[]{:S(2)}, u32[]{:S(2)}) collective-permute-start(f32[128,512]{1,0:T(8,128)S(1)} %shard_map.51.own), channel_id=1, source_target_pairs={{0,16},{8,24},{16,0},{24,8},{1,17},{9,25},{17,1},{25,9},{2,18},{10... | collective-permute-start | bytes 786440 | tf_op jit(solution)/shard_map/ppermute | solution.py:294
  39.3 0.7 fusion.31.refs_11_.refs_9_
  40.0 0.8 fusion.33.refs_13_.refs_11_
  40.8 5.7 %collective-permute-done.2.got = f32[128,512]{1,0:T(8,128)S(1)} collective-permute-done((f32[128,512]{1,0:T(8,128)S(1)}, f32[128,512]{1,0:T(8,128)S(1)}, u32[]{:S(2)}, u32[]{:S(2)}) %collective-permute-start.2) | collective-permute-done | bytes 262176 | tf_op jit(solution)/shard_map/ppermute | solution.py:294
  46.5 0.4 collective-permute-start.3
  46.9 1.7 %collective-permute-start.4 = (f32[32,512]{1,0:T(8,128)S(1)}, f32[32,512]{1,0:T(8,128)S(1)}, u32[]{:S(2)}, u32[]{:S(2)}) collective-permute-start(f32[32,512]{1,0:T(8,128)S(1)} %get-tuple-element.32), channel_id=1, source_target_pairs={{0,2},{1,3},{2,0},{3,1},{4,6},{5,7},{6,4},{7,5},{8,10},{9,11},{10,... | collective-permute-start | bytes 196616 | tf_op jit(solution)/shard_map/ppermute | solution.py:287
  48.7 1.4 %collective-permute-start.5 = (f32[32,512]{1,0:T(8,128)S(1)}, f32[32,512]{1,0:T(8,128)S(1)}, u32[]{:S(2)}, u32[]{:S(2)}) collective-permute-start(f32[32,512]{1,0:T(8,128)S(1)} %get-tuple-element.33), channel_id=1, source_target_pairs={{0,3},{1,2},{2,1},{3,0},{4,7},{5,6},{6,5},{7,4},{8,11},{9,10},{10,... | collective-permute-start | bytes 196616 | tf_op jit(solution)/shard_map/ppermute | solution.py:287
  50.1 0.7 fusion.37.refs_3_.refs_13_
  50.8 0.4 collective-permute-done.4.refs_2_
  51.2 2.6 %collective-permute-done.5.refs_3_ = f32[32,512]{1,0:T(8,128)S(1)} collective-permute-done((f32[32,512]{1,0:T(8,128)S(1)}, f32[32,512]{1,0:T(8,128)S(1)}, u32[]{:S(2)}, u32[]{:S(2)}) %collective-permute-start.5) | collective-permute-done | bytes 65568 | tf_op jit(solution)/shard_map/ppermute | solution.py:287
  53.8 1.8 %shard_map.56 = (f32[32,2048]{1,0:T(8,128)S(1)}, bf16[32,512]{1,0:T(8,128)(2,1)S(1)}, f32[32,2048]{1,0:T(8,128)S(1)}) custom-call(f32[32,512]{1,0:T(8,128)S(1)} %get-tuple-element.30.refs_0_, f32[32,512]{1,0:T(8,128)S(1)} %collective-permute-done.3.refs_1_, f32[32,512]{1,0:T(8,128)S(1)} %collective-permute-done.4.refs_2_, ...), custom_call_target="tpu_custom_call" | custom-call | flops 1610612736 | tf_op jit(solution)/shard_map/pallas_call | solution.py:384
  55.7 0.8 shard_map.58
  56.4 2.6 %collective-permute-start.15 = (bf16[32,2048]{1,0:T(8,128)(2,1)S(1)}, bf16[32,2048]{1,0:T(8,128)(2,1)S(1)}, u32[]{:S(2)}, u32[]{:S(2)}) collective-permute-start(bf16[32,2048]{1,0:T(8,128)(2,1)S(1)} %get-tuple-element.43), channel_id=1, source_target_pairs={{0,4},{1,5},{2,6},{3,7},{4,0},{5,1},{6,2},{7,3},{8,12},{9,13},{10,... | collective-permute-start | bytes 393224 | tf_op jit(solution)/shard_map/ppermute | solution.py:294
  59.1 4.8 %collective-permute-done.15.got = bf16[32,2048]{1,0:T(8,128)(2,1)S(1)} collective-permute-done((bf16[32,2048]{1,0:T(8,128)(2,1)S(1)}, bf16[32,2048]{1,0:T(8,128)(2,1)S(1)}, u32[]{:S(2)}, u32[]{:S(2)}) %collective-permute-start.15) | collective-permute-done | bytes 131104 | tf_op jit(solution)/shard_map/ppermute | solution.py:294
  63.9 1.5 %shard_map.59.own = f32[32,2048]{1,0:T(8,128)S(1)} custom-call(f32[32,2048]{1,0:T(8,128)S(1)} %get-tuple-element.42.partial, bf16[32,2048]{1,0:T(8,128)(2,1)S(1)} %collective-permute-done.15.got, bf16[1024,512]{1,0:T(8,128)(2,1)S(1)} %fusion.refs_0_.refs_4_, bf16[1024,256]{1,0:T(8,128)(2,1)S(1)} %fusion.26.refs_5_.refs_1_, ...), custom_call_target="tpu_custom_call" | custom-call | flops 2147483648 | tf_op jit(solution)/shard_map/pallas_call | solution.py:399
  65.4 1.5 %collective-permute-start.16 = (f32[32,2048]{1,0:T(8,128)S(1)}, f32[32,2048]{1,0:T(8,128)S(1)}, u32[]{:S(2)}, u32[]{:S(2)}) collective-permute-start(f32[32,2048]{1,0:T(8,128)S(1)} %shard_map.59.own), channel_id=1, source_target_pairs={{0,16},{8,24},{16,0},{24,8},{1,17},{9,25},{17,1},{25,9},{2,18},{10... | collective-permute-start | bytes 786440 | tf_op jit(solution)/shard_map/ppermute | solution.py:294
  66.9 4.9 %collective-permute-done.16.got = f32[32,2048]{1,0:T(8,128)S(1)} collective-permute-done((f32[32,2048]{1,0:T(8,128)S(1)}, f32[32,2048]{1,0:T(8,128)S(1)}, u32[]{:S(2)}, u32[]{:S(2)}) %collective-permute-start.16) | collective-permute-done | bytes 262176 | tf_op jit(solution)/shard_map/ppermute | solution.py:294
  71.8 0.2 shard_map.60
  72.0 1.1 %collective-permute-start.17 = (f32[3,32,128]{2,1,0:T(8,128)S(1)}, f32[3,32,128]{2,1,0:T(8,128)S(1)}, u32[]{:S(2)}, u32[]{:S(2)}) collective-permute-start(f32[3,32,128]{2,1,0:T(8,128)S(1)} %get-tuple-element.45.own_sums), channel_id=1, source_target_pairs={{0,4},{1,5},{2,6},{3,7},{4,0},{5,1},{6,2},{7,3},{8,12},{9,13},{10,... | collective-permute-start | bytes 147464 | tf_op jit(solution)/shard_map/ppermute | solution.py:294
  73.1 4.3 %collective-permute-done.17.got_sums = f32[3,32,128]{2,1,0:T(8,128)S(1)} collective-permute-done((f32[3,32,128]{2,1,0:T(8,128)S(1)}, f32[3,32,128]{2,1,0:T(8,128)S(1)}, u32[]{:S(2)}, u32[]{:S(2)}) %collective-permute-start.17) | collective-permute-done | bytes 49184 | tf_op jit(solution)/shard_map/ppermute | solution.py:294
  77.4 2.7 %shard_map.61 = (f32[32,2048]{1,0:T(8,128)S(1)}, f32[32,2048]{1,0:T(8,128)S(1)}, f32[32,2048]{1,0:T(8,128)S(1)}, bf16[32,2048]{1,0:T(8,128)(2,1)S(1)}) custom-call(f32[3,32,128]{2,1,0:T(8,128)S(1)} %get-tuple-element.45.own_sums, f32[3,32,128]{2,1,0:T(8,128)S(1)} %collective-permute-done.17.got_sums, f32[32,2048]{1,0:T(8,128)S(1)} %get-tuple-element.44.right_side, ...), custom_call_target="tpu_custom_call" | custom-call | flops 2147483648 | tf_op jit(solution)/shard_map/pallas_call | solution.py:407
  80.1 0.8 collective-permute-start.18
  80.9 6.1 %collective-permute-done.18.got = bf16[32,2048]{1,0:T(8,128)(2,1)S(1)} collective-permute-done((bf16[32,2048]{1,0:T(8,128)(2,1)S(1)}, bf16[32,2048]{1,0:T(8,128)(2,1)S(1)}, u32[]{:S(2)}, u32[]{:S(2)}) %collective-permute-start.18) | collective-permute-done | bytes 131104 | tf_op jit(solution)/shard_map/ppermute | solution.py:294
  86.9 1.5 %shard_map.62 = (f32[32,2048]{1,0:T(8,128)S(1)}, bf16[32,2048]{1,0:T(8,128)(2,1)S(1)}, f32[32,128]{1,0:T(8,128)S(1)}) custom-call(f32[32,2048]{1,0:T(8,128)S(1)} %get-tuple-element.47.partial, bf16[32,2048]{1,0:T(8,128)(2,1)S(1)} %collective-permute-done.18.got, bf16[1024,512]{1,0:T(8,128)(2,1)S(1)} %fusion.refs_0_.refs_4_, ...), custom_call_target="tpu_custom_call" | custom-call | flops 2147483648 | tf_op jit(solution)/shard_map/pallas_call | solution.py:411
  88.5 1.5 %collective-permute-start.20 = (bf16[32,2048]{1,0:T(8,128)(2,1)S(1)}, bf16[32,2048]{1,0:T(8,128)(2,1)S(1)}, u32[]{:S(2)}, u32[]{:S(2)}) collective-permute-start(bf16[32,2048]{1,0:T(8,128)(2,1)S(1)} %get-tuple-element.51), channel_id=1, source_target_pairs={{0,16},{8,24},{16,0},{24,8},{1,17},{9,25},{17,1},{25,9},{2,18},{10... | collective-permute-start | bytes 393224 | tf_op jit(solution)/shard_map/ppermute | solution.py:294
  89.9 0.6 collective-permute-start.19
  90.5 3.2 %collective-permute-done.19.got_sq = f32[32,128]{1,0:T(8,128)S(1)} collective-permute-done((f32[32,128]{1,0:T(8,128)S(1)}, f32[32,128]{1,0:T(8,128)S(1)}, u32[]{:S(2)}, u32[]{:S(2)}) %collective-permute-start.19) | collective-permute-done | bytes 16416 | tf_op jit(solution)/shard_map/ppermute | solution.py:294
  93.7 0.2 shard_map.63
  93.9 1.3 %collective-permute-start.21 = (bf16[64,512]{1,0:T(8,128)(2,1)S(1)}, bf16[64,512]{1,0:T(8,128)(2,1)S(1)}, u32[]{:S(2)}, u32[]{:S(2)}) collective-permute-start(bf16[64,512]{1,0:T(8,128)(2,1)S(1)} %get-tuple-element.55), channel_id=1, source_target_pairs={{0,1},{1,0},{2,3},{3,2},{4,5},{5,4},{6,7},{7,6},{8,9},{9,8},{10,11... | collective-permute-start | bytes 196616 | tf_op jit(solution)/shard_map/ppermute | solution.py:287
  95.2 2.2 %collective-permute-start.23 = (bf16[64,512]{1,0:T(8,128)(2,1)S(1)}, bf16[64,512]{1,0:T(8,128)(2,1)S(1)}, u32[]{:S(2)}, u32[]{:S(2)}) collective-permute-start(bf16[64,512]{1,0:T(8,128)(2,1)S(1)} %get-tuple-element.57), channel_id=1, source_target_pairs={{0,3},{1,2},{2,1},{3,0},{4,7},{5,6},{6,5},{7,4},{8,11},{9,10},{10,... | collective-permute-start | bytes 196616 | tf_op jit(solution)/shard_map/ppermute | solution.py:287
  97.4 0.8 collective-permute-done.21.refs_1_
  98.2 1.3 %collective-permute-done.22.refs_2_ = bf16[64,512]{1,0:T(8,128)(2,1)S(1)} collective-permute-done((bf16[64,512]{1,0:T(8,128)(2,1)S(1)}, bf16[64,512]{1,0:T(8,128)(2,1)S(1)}, u32[]{:S(2)}, u32[]{:S(2)}) %collective-permute-start.22) | collective-permute-done | bytes 65568 | tf_op jit(solution)/shard_map/ppermute | solution.py:287
  99.5 0.9 collective-permute-done.23.refs_3_
  100.5 0.3 collective-permute-done.26.refs_6_
  100.7 0.9 collective-permute-done.27.refs_7_
  101.6 1.8 %shard_map.64 = (f32[512,256]{1,0:T(8,128)}, f32[512,256]{1,0:T(8,128)}) custom-call(s32[2]{0:T(128)S(1)} %pad_add_fusion.place, bf16[64,512]{1,0:T(8,128)(2,1)S(1)} %get-tuple-element.54.refs_0_, bf16[64,512]{1,0:T(8,128)(2,1)S(1)} %collective-permute-done.21.refs_1_, bf16[64,512]{1,0:T(8,128)(2,1)S(1)} %collective-permute-done.22.refs_2_, ...), custom_call_target="tpu_custom_call" | custom-call | flops 1000000 | tf_op jit(solution)/shard_map/pallas_call | solution.py:423
  (33 shorter events, 0.6 us)
Async XLA Ops:
  0.6 10.4 %copy-start = (bf16[1024,256]{1,0:T(8,128)(2,1)S(1)}, bf16[1024,256]{1,0:T(8,128)(2,1)}, u32[]{:S(2)}) copy-start(bf16[1024,256]{1,0:T(8,128)(2,1)} %param.5) | copy-start | bytes 1572868
  2.6 10.4 %collective-permute-start.6 = (bf16[128,1024]{1,0:T(8,128)(2,1)}, bf16[128,1024]{1,0:T(8,128)(2,1)S(1)}, u32[]{:S(2)}, u32[]{:S(2)}) collective-permute-start(bf16[128,1024]{1,0:T(8,128)(2,1)} %get-tuple-element.34), channel_id=1, source_target_pairs={{0,1},{1,0},{2,3},{3,2},{4,5},{5,4},{6,7},{7,6},{8,9},{9,8},{10,11... | collective-permute-start | bytes 786440 | tf_op jit(solution)/shard_map/ppermute | solution.py:287
  5.6 9.4 %collective-permute-start.7 = (bf16[128,1024]{1,0:T(8,128)(2,1)}, bf16[128,1024]{1,0:T(8,128)(2,1)S(1)}, u32[]{:S(2)}, u32[]{:S(2)}) collective-permute-start(bf16[128,1024]{1,0:T(8,128)(2,1)} %get-tuple-element.34), channel_id=1, source_target_pairs={{0,2},{1,3},{2,0},{3,1},{4,6},{5,7},{6,4},{7,5},{8,10},{9,11},{10,... | collective-permute-start | bytes 786440 | tf_op jit(solution)/shard_map/ppermute | solution.py:287
  7.2 12.0 %collective-permute-start.10 = (bf16[128,1024]{1,0:T(8,128)(2,1)}, bf16[128,1024]{1,0:T(8,128)(2,1)S(1)}, u32[]{:S(2)}, u32[]{:S(2)}) collective-permute-start(bf16[128,1024]{1,0:T(8,128)(2,1)} %get-tuple-element.36), channel_id=1, source_target_pairs={{0,2},{1,3},{2,0},{3,1},{4,6},{5,7},{6,4},{7,5},{8,10},{9,11},{10,... | collective-permute-start | bytes 786440 | tf_op jit(solution)/shard_map/ppermute | solution.py:287
  7.6 11.9 %collective-permute-start.9 = (bf16[128,1024]{1,0:T(8,128)(2,1)}, bf16[128,1024]{1,0:T(8,128)(2,1)S(1)}, u32[]{:S(2)}, u32[]{:S(2)}) collective-permute-start(bf16[128,1024]{1,0:T(8,128)(2,1)} %get-tuple-element.36), channel_id=1, source_target_pairs={{0,1},{1,0},{2,3},{3,2},{4,5},{5,4},{6,7},{7,6},{8,9},{9,8},{10,11... | collective-permute-start | bytes 786440 | tf_op jit(solution)/shard_map/ppermute | solution.py:287
  7.7 24.1 %collective-permute-start.1 = (bf16[1024,1024]{1,0:T(8,128)(2,1)}, bf16[1024,1024]{1,0:T(8,128)(2,1)}, u32[]{:S(2)}, u32[]{:S(2)}) collective-permute-start(bf16[1024,1024]{1,0:T(8,128)(2,1)} %param.3), channel_id=1, source_target_pairs={{0,8},{8,0},{16,24},{24,16},{1,9},{9,1},{17,25},{25,17},{2,10},{10... | collective-permute-start | bytes 6291464 | tf_op jit(solution)/shard_map/ppermute | solution.py:284
  13.0 24.3 %collective-permute-start = (bf16[128,1024]{1,0:T(8,128)(2,1)S(1)}, bf16[128,1024]{1,0:T(8,128)(2,1)S(1)}, u32[]{:S(2)}, u32[]{:S(2)}) collective-permute-start(bf16[128,1024]{1,0:T(8,128)(2,1)S(1)} %convolution_convert_fusion), channel_id=1, source_target_pairs={{0,8},{8,0},{16,24},{24,16},{1,9},{9,1},{17,25},{25,17},{2,10},{10... | collective-permute-start | bytes 786440 | tf_op jit(solution)/shard_map/ppermute | solution.py:284
  15.1 14.4 %collective-permute-start.8 = (bf16[256,1024]{1,0:T(8,128)(2,1)S(1)}, bf16[256,1024]{1,0:T(8,128)(2,1)S(1)}, u32[]{:S(2)}, u32[]{:S(2)}) collective-permute-start(bf16[256,1024]{1,0:T(8,128)(2,1)S(1)} %get-tuple-element.35), channel_id=1, source_target_pairs={{0,8},{8,0},{16,24},{24,16},{1,9},{9,1},{17,25},{25,17},{2,10},{10... | collective-permute-start | bytes 1572872 | tf_op jit(solution)/shard_map/ppermute | solution.py:284
  19.2 6.4 %collective-permute-start.12 = (bf16[128,1024]{1,0:T(8,128)(2,1)S(1)}, bf16[128,1024]{1,0:T(8,128)(2,1)S(1)}, u32[]{:S(2)}, u32[]{:S(2)}) collective-permute-start(bf16[128,1024]{1,0:T(8,128)(2,1)S(1)} %get-tuple-element.40), channel_id=1, source_target_pairs={{0,1},{1,0},{2,3},{3,2},{4,5},{5,4},{6,7},{7,6},{8,10},{9,11},{10,... | collective-permute-start | bytes 786440 | tf_op jit(solution)/shard_map/ppermute | solution.py:363
  19.7 4.1 %copy-start.2 = (bf16[1024,1024]{1,0:T(8,128)(2,1)S(1)}, bf16[1024,1024]{1,0:T(8,128)(2,1)}, u32[]{:S(2)}) copy-start(bf16[1024,1024]{1,0:T(8,128)(2,1)} %param.3) | copy-start | bytes 6291460
  19.7 8.7 %collective-permute-start.13 = (bf16[128,1024]{1,0:T(8,128)(2,1)S(1)}, bf16[128,1024]{1,0:T(8,128)(2,1)S(1)}, u32[]{:S(2)}, u32[]{:S(2)}) collective-permute-start(bf16[128,1024]{1,0:T(8,128)(2,1)S(1)} %get-tuple-element.41), channel_id=1, source_target_pairs={{0,1},{1,0},{2,3},{3,2},{4,5},{5,4},{6,7},{7,6},{8,10},{9,11},{10,... | collective-permute-start | bytes 786440 | tf_op jit(solution)/shard_map/ppermute | solution.py:363
  25.6 4.7 %collective-permute-start.11 = (bf16[256,1024]{1,0:T(8,128)(2,1)S(1)}, bf16[256,1024]{1,0:T(8,128)(2,1)S(1)}, u32[]{:S(2)}, u32[]{:S(2)}) collective-permute-start(bf16[256,1024]{1,0:T(8,128)(2,1)S(1)} %get-tuple-element.37), channel_id=1, source_target_pairs={{0,8},{8,0},{16,24},{24,16},{1,9},{9,1},{17,25},{25,17},{2,10},{10... | collective-permute-start | bytes 1572872 | tf_op jit(solution)/shard_map/ppermute | solution.py:284
  28.6 2.4 %collective-permute-start.14 = (bf16[256,1024]{1,0:T(8,128)(2,1)S(1)}, bf16[256,1024]{1,0:T(8,128)(2,1)S(1)}, u32[]{:S(2)}, u32[]{:S(2)}) collective-permute-start(bf16[256,1024]{1,0:T(8,128)(2,1)S(1)} %shard_map.57), channel_id=1, source_target_pairs={{0,8},{8,0},{16,24},{24,16},{1,9},{9,1},{17,25},{25,17},{2,10},{10... | collective-permute-start | bytes 1572872 | tf_op jit(solution)/shard_map/ppermute | solution.py:284
  31.8 1.9 %copy-start.1 = (bf16[512,1024]{1,0:T(8,128)(2,1)S(1)}, bf16[512,1024]{1,0:T(8,128)(2,1)}, u32[]{:S(2)}) copy-start(bf16[512,1024]{1,0:T(8,128)(2,1)} %centers.1) | copy-start | bytes 3145732
  37.7 8.8 %collective-permute-start.2 = (f32[128,512]{1,0:T(8,128)S(1)}, f32[128,512]{1,0:T(8,128)S(1)}, u32[]{:S(2)}, u32[]{:S(2)}) collective-permute-start(f32[128,512]{1,0:T(8,128)S(1)} %shard_map.51.own), channel_id=1, source_target_pairs={{0,16},{8,24},{16,0},{24,8},{1,17},{9,25},{17,1},{25,9},{2,18},{10... | collective-permute-start | bytes 786440 | tf_op jit(solution)/shard_map/ppermute | solution.py:294
  46.5 4.3 %collective-permute-start.3 = (f32[32,512]{1,0:T(8,128)S(1)}, f32[32,512]{1,0:T(8,128)S(1)}, u32[]{:S(2)}, u32[]{:S(2)}) collective-permute-start(f32[32,512]{1,0:T(8,128)S(1)} %get-tuple-element.31), channel_id=1, source_target_pairs={{0,1},{1,0},{2,3},{3,2},{4,5},{5,4},{6,7},{7,6},{8,9},{9,8},{10,11... | collective-permute-start | bytes 196616 | tf_op jit(solution)/shard_map/ppermute | solution.py:287
  46.9 4.3 %collective-permute-start.4 = (f32[32,512]{1,0:T(8,128)S(1)}, f32[32,512]{1,0:T(8,128)S(1)}, u32[]{:S(2)}, u32[]{:S(2)}) collective-permute-start(f32[32,512]{1,0:T(8,128)S(1)} %get-tuple-element.32), channel_id=1, source_target_pairs={{0,2},{1,3},{2,0},{3,1},{4,6},{5,7},{6,4},{7,5},{8,10},{9,11},{10,... | collective-permute-start | bytes 196616 | tf_op jit(solution)/shard_map/ppermute | solution.py:287
  48.7 5.2 %collective-permute-start.5 = (f32[32,512]{1,0:T(8,128)S(1)}, f32[32,512]{1,0:T(8,128)S(1)}, u32[]{:S(2)}, u32[]{:S(2)}) collective-permute-start(f32[32,512]{1,0:T(8,128)S(1)} %get-tuple-element.33), channel_id=1, source_target_pairs={{0,3},{1,2},{2,1},{3,0},{4,7},{5,6},{6,5},{7,4},{8,11},{9,10},{10,... | collective-permute-start | bytes 196616 | tf_op jit(solution)/shard_map/ppermute | solution.py:287
  56.4 7.5 %collective-permute-start.15 = (bf16[32,2048]{1,0:T(8,128)(2,1)S(1)}, bf16[32,2048]{1,0:T(8,128)(2,1)S(1)}, u32[]{:S(2)}, u32[]{:S(2)}) collective-permute-start(bf16[32,2048]{1,0:T(8,128)(2,1)S(1)} %get-tuple-element.43), channel_id=1, source_target_pairs={{0,4},{1,5},{2,6},{3,7},{4,0},{5,1},{6,2},{7,3},{8,12},{9,13},{10,... | collective-permute-start | bytes 393224 | tf_op jit(solution)/shard_map/ppermute | solution.py:294
  65.4 6.4 %collective-permute-start.16 = (f32[32,2048]{1,0:T(8,128)S(1)}, f32[32,2048]{1,0:T(8,128)S(1)}, u32[]{:S(2)}, u32[]{:S(2)}) collective-permute-start(f32[32,2048]{1,0:T(8,128)S(1)} %shard_map.59.own), channel_id=1, source_target_pairs={{0,16},{8,24},{16,0},{24,8},{1,17},{9,25},{17,1},{25,9},{2,18},{10... | collective-permute-start | bytes 786440 | tf_op jit(solution)/shard_map/ppermute | solution.py:294
  72.0 5.4 %collective-permute-start.17 = (f32[3,32,128]{2,1,0:T(8,128)S(1)}, f32[3,32,128]{2,1,0:T(8,128)S(1)}, u32[]{:S(2)}, u32[]{:S(2)}) collective-permute-start(f32[3,32,128]{2,1,0:T(8,128)S(1)} %get-tuple-element.45.own_sums), channel_id=1, source_target_pairs={{0,4},{1,5},{2,6},{3,7},{4,0},{5,1},{6,2},{7,3},{8,12},{9,13},{10,... | collective-permute-start | bytes 147464 | tf_op jit(solution)/shard_map/ppermute | solution.py:294
  80.1 6.8 %collective-permute-start.18 = (bf16[32,2048]{1,0:T(8,128)(2,1)S(1)}, bf16[32,2048]{1,0:T(8,128)(2,1)S(1)}, u32[]{:S(2)}, u32[]{:S(2)}) collective-permute-start(bf16[32,2048]{1,0:T(8,128)(2,1)S(1)} %get-tuple-element.48), channel_id=1, source_target_pairs={{0,4},{1,5},{2,6},{3,7},{4,0},{5,1},{6,2},{7,3},{8,12},{9,13},{10,... | collective-permute-start | bytes 393224 | tf_op jit(solution)/shard_map/ppermute | solution.py:294
  88.5 5.2 %collective-permute-start.20 = (bf16[32,2048]{1,0:T(8,128)(2,1)S(1)}, bf16[32,2048]{1,0:T(8,128)(2,1)S(1)}, u32[]{:S(2)}, u32[]{:S(2)}) collective-permute-start(bf16[32,2048]{1,0:T(8,128)(2,1)S(1)} %get-tuple-element.51), channel_id=1, source_target_pairs={{0,16},{8,24},{16,0},{24,8},{1,17},{9,25},{17,1},{25,9},{2,18},{10... | collective-permute-start | bytes 393224 | tf_op jit(solution)/shard_map/ppermute | solution.py:294
  89.9 3.7 %collective-permute-start.19 = (f32[32,128]{1,0:T(8,128)S(1)}, f32[32,128]{1,0:T(8,128)S(1)}, u32[]{:S(2)}, u32[]{:S(2)}) collective-permute-start(f32[32,128]{1,0:T(8,128)S(1)} %get-tuple-element.49.own_sq), channel_id=1, source_target_pairs={{0,16},{8,24},{16,0},{24,8},{1,17},{9,25},{17,1},{25,9},{2,18},{10... | collective-permute-start | bytes 49160 | tf_op jit(solution)/shard_map/ppermute | solution.py:294
  93.9 4.3 %collective-permute-start.21 = (bf16[64,512]{1,0:T(8,128)(2,1)S(1)}, bf16[64,512]{1,0:T(8,128)(2,1)S(1)}, u32[]{:S(2)}, u32[]{:S(2)}) collective-permute-start(bf16[64,512]{1,0:T(8,128)(2,1)S(1)} %get-tuple-element.55), channel_id=1, source_target_pairs={{0,1},{1,0},{2,3},{3,2},{4,5},{5,4},{6,7},{7,6},{8,9},{9,8},{10,11... | collective-permute-start | bytes 196616 | tf_op jit(solution)/shard_map/ppermute | solution.py:287
  95.2 4.3 %collective-permute-start.22 = (bf16[64,512]{1,0:T(8,128)(2,1)S(1)}, bf16[64,512]{1,0:T(8,128)(2,1)S(1)}, u32[]{:S(2)}, u32[]{:S(2)}) collective-permute-start(bf16[64,512]{1,0:T(8,128)(2,1)S(1)} %get-tuple-element.56), channel_id=1, source_target_pairs={{0,2},{1,3},{2,0},{3,1},{4,6},{5,7},{6,4},{7,5},{8,10},{9,11},{10,... | collective-permute-start | bytes 196616 | tf_op jit(solution)/shard_map/ppermute | solution.py:287
  95.2 5.2 %collective-permute-start.23 = (bf16[64,512]{1,0:T(8,128)(2,1)S(1)}, bf16[64,512]{1,0:T(8,128)(2,1)S(1)}, u32[]{:S(2)}, u32[]{:S(2)}) collective-permute-start(bf16[64,512]{1,0:T(8,128)(2,1)S(1)} %get-tuple-element.57), channel_id=1, source_target_pairs={{0,3},{1,2},{2,1},{3,0},{4,7},{5,6},{6,5},{7,4},{8,11},{9,10},{10,... | collective-permute-start | bytes 196616 | tf_op jit(solution)/shard_map/ppermute | solution.py:287
  97.4 3.0 %collective-permute-start.24 = (bf16[64,512]{1,0:T(8,128)(2,1)S(1)}, bf16[64,512]{1,0:T(8,128)(2,1)S(1)}, u32[]{:S(2)}, u32[]{:S(2)}) collective-permute-start(bf16[64,512]{1,0:T(8,128)(2,1)S(1)} %get-tuple-element.54.refs_0_), channel_id=1, source_target_pairs={{0,8},{8,0},{16,24},{24,16},{1,9},{9,1},{17,25},{25,17},{2,10},{10... | collective-permute-start | bytes 196616 | tf_op jit(solution)/shard_map/ppermute | solution.py:284
  98.2 2.3 %collective-permute-start.25 = (bf16[64,512]{1,0:T(8,128)(2,1)S(1)}, bf16[64,512]{1,0:T(8,128)(2,1)S(1)}, u32[]{:S(2)}, u32[]{:S(2)}) collective-permute-start(bf16[64,512]{1,0:T(8,128)(2,1)S(1)} %collective-permute-done.21.refs_1_), channel_id=1, source_target_pairs={{0,8},{8,0},{16,24},{24,16},{1,9},{9,1},{17,25},{25,17},{2,10},{10... | collective-permute-start | bytes 196616 | tf_op jit(solution)/shard_map/ppermute | solution.py:284
  99.5 1.3 %collective-permute-start.26 = (bf16[64,512]{1,0:T(8,128)(2,1)S(1)}, bf16[64,512]{1,0:T(8,128)(2,1)S(1)}, u32[]{:S(2)}, u32[]{:S(2)}) collective-permute-start(bf16[64,512]{1,0:T(8,128)(2,1)S(1)} %collective-permute-done.22.refs_2_), channel_id=1, source_target_pairs={{0,8},{8,0},{16,24},{24,16},{1,9},{9,1},{17,25},{25,17},{2,10},{10... | collective-permute-start | bytes 196616 | tf_op jit(solution)/shard_map/ppermute | solution.py:284
  100.4 1.3 %collective-permute-start.27 = (bf16[64,512]{1,0:T(8,128)(2,1)S(1)}, bf16[64,512]{1,0:T(8,128)(2,1)S(1)}, u32[]{:S(2)}, u32[]{:S(2)}) collective-permute-start(bf16[64,512]{1,0:T(8,128)(2,1)S(1)} %collective-permute-done.23.refs_3_), channel_id=1, source_target_pairs={{0,8},{8,0},{16,24},{24,16},{1,9},{9,1},{17,25},{25,17},{2,10},{10... | collective-permute-start | bytes 196616 | tf_op jit(solution)/shard_map/ppermute | solution.py:284
